TPU v7x, 256 devices: a whole 4x4x8 slice. The times are simulated.
256 devices in a mesh: ha: 8 (over z_hi, core), wa: 8 (over z_lo, y), ba: 4 (over x).
Axes of the slice: x: 4, y: 4, z: 8 (z_hi: 4, z_lo: 2; z = z_hi * 2 + z_lo), core: 2. Of those that a mesh axis runs over, the one named last changes fastest.
Arguments:
- tokens: bfloat16 [32, 64, 64, 512], P('ba', 'ha', 'wa'), parts along dimension 0, may hold values from -6 to 6
- norm_gain: float32 [3, 512], replicated, may hold values from 0.1 to 1.9
- w_gatevals: bfloat16 [3, 512, 2048], replicated, may hold values from -0.25 to 0.25
- w_coupling: bfloat16 [3, 512, 128], replicated, may hold values from -0.25 to 0.25
- w_steps: bfloat16 [3, 512, 16], replicated, may hold values from -0.25 to 0.25
- conv_values: float32 [3, 4, 1024], replicated, may hold values from -3 to 3
- conv_coupling: float32 [3, 4, 128], replicated, may hold values from -3 to 3
- step_bias: float32 [3, 16], replicated, may hold values from -4 to 0
- rate_log: float32 [3, 16], replicated, may hold values from -1.5 to 1.5
- skip_gain: float32 [3, 16], replicated, may hold values from 0.5 to 2
- out_gain: float32 [3, 1024], replicated, may hold values from 0.1 to 1.9
- w_output: bfloat16 [3, 1024, 512], replicated, may hold values from -0.1875 to 0.1875
Outputs:
- result: bfloat16 [32, 64, 64, 512], P('ba', 'ha', 'wa'), parts along dimension 0
There are 4 independent parts, one for each index of `ba`. A program takes and returns all parts, laid end to end along the dimension named above; an argument that names none is the same for every part. Nothing has to cross between parts.
All inputs are finite; a program needn't handle non-finite values.
Results may differ from a plain program's by a relative error of at most 0.025.
Values may be sent and summed in bfloat16 or wider, within the bound.
No kernel may reach another device: no remote copies, remote signals or barrier semaphores. Data moves between devices by JAX's collectives and lax.ppermute only.
A program may use at most 128 MiB of HBM per device.

v0:
```python
import jax
import jax.numpy as jnp
from jax import lax
from jax.sharding import PartitionSpec as P


def cut_along(shard, dim, devices):
    shape = shard.shape
    tiles = shard.reshape(*shape[:dim], devices, shape[dim] // devices, *shape[dim + 1 :])
    return jnp.moveaxis(tiles, dim, 0)


def in_order(tiles, dim):
    shape = list(tiles.shape[1:])
    shape[dim] *= tiles.shape[0]
    return jnp.moveaxis(tiles, 0, dim).reshape(shape)


def one_exchange(shard, axis, axes, splits, concats):
    sizes = [lax.axis_size(a) for a in axes]
    tiles = cut_along(shard, splits[0], sizes[0])
    tiles = jnp.moveaxis(cut_along(tiles, splits[1] + 1, sizes[1]), 0, 1)
    inside = tiles.shape[2:]
    tiles = tiles.reshape(-1, *inside)
    tiles = lax.all_to_all(tiles, axis, split_axis=0, concat_axis=0, tiled=True)
    tiles = in_order(tiles.reshape(*sizes, *inside), concats[0] + 1)
    return in_order(tiles, concats[1])


def causal_conv(values, kernel):
    length = values.shape[1]
    taps = kernel.shape[0]
    padded = jnp.pad(values, ((0, 0), (taps - 1, 0), (0, 0)))
    total = jnp.zeros_like(values)
    for offset in range(taps):
        total = total + padded[:, offset : offset + length, :] * kernel[offset]
    return total


def mixer(stream, params):
    (
        norm_gain,
        w_gatevals,
        w_coupling,
        w_steps,
        conv_values,
        conv_coupling,
        step_bias,
        rate_log,
        skip_gain,
        out_gain,
        w_output,
    ) = params
    count, length, width = stream.shape
    inner = w_gatevals.shape[1] // 2
    states = w_coupling.shape[1] // 2
    heads = w_steps.shape[1]
    headdim = inner // heads
    flat = stream.reshape(count * length, width).astype(jnp.float32)
    normed = (
        flat * lax.rsqrt(jnp.mean(flat * flat, axis=-1, keepdims=True) + 1e-05) * norm_gain
    ).astype(jnp.bfloat16)
    gatevals = jnp.dot(normed, w_gatevals, preferred_element_type=jnp.float32).astype(jnp.bfloat16)
    coupling = jnp.dot(normed, w_coupling, preferred_element_type=jnp.float32).astype(jnp.bfloat16)
    step_raw = jnp.dot(normed, w_steps, preferred_element_type=jnp.float32)
    gate = gatevals[:, :inner]
    values = gatevals[:, inner:]
    xs = jax.nn.silu(
        causal_conv(values.astype(jnp.float32).reshape(count, length, inner), conv_values)
    ).astype(jnp.bfloat16)
    maps = jax.nn.silu(
        causal_conv(coupling.astype(jnp.float32).reshape(count, length, 2 * states), conv_coupling)
    ).astype(jnp.bfloat16)
    input_map = maps[:, :, :states]
    output_map = maps[:, :, states:]
    steps = jax.nn.softplus(step_raw.reshape(count, length, heads) + step_bias)
    cumul = jnp.cumsum(steps * -jnp.exp(rate_log), axis=1).transpose(0, 2, 1)
    steps_heads = steps.transpose(0, 2, 1)
    positions = jnp.arange(length, dtype=jnp.int32)
    lower = positions[:, None] >= positions[None, :]
    spread = cumul[:, :, :, None] - cumul[:, :, None, :]
    decay = jnp.exp(jnp.where(lower[None, None, :, :], spread, -jnp.inf))
    scores = jnp.einsum("ntk,nsk->nts", output_map, input_map, preferred_element_type=jnp.float32)
    weights = (scores[:, None, :, :] * decay * steps_heads[:, :, None, :]).astype(jnp.bfloat16)
    heads_in = xs.reshape(count, length, heads, headdim)
    mixed = jnp.einsum("nhts,nshp->nthp", weights, heads_in, preferred_element_type=jnp.float32)
    mixed = mixed + skip_gain[:, None] * heads_in.astype(jnp.float32)
    gated = mixed.reshape(count * length, inner) * jax.nn.silu(gate.astype(jnp.float32))
    normal = (
        gated * lax.rsqrt(jnp.mean(gated * gated, axis=-1, keepdims=True) + 1e-05) * out_gain
    ).astype(jnp.bfloat16)
    update = jnp.dot(normal, w_output, preferred_element_type=jnp.float32)
    return (flat + update).astype(jnp.bfloat16).reshape(count, length, width)


def shards(
    tokens,
    norm_gain,
    w_gatevals,
    w_coupling,
    w_steps,
    conv_values,
    conv_coupling,
    step_bias,
    rate_log,
    skip_gain,
    out_gain,
    w_output,
):
    stacked = (
        norm_gain,
        w_gatevals,
        w_coupling,
        w_steps,
        conv_values,
        conv_coupling,
        step_bias,
        rate_log,
        skip_gain,
        out_gain,
        w_output,
    )

    def params_of(index):
        return tuple((member[index] for member in stacked))

    frames, rows_dev, cols_dev, width = tokens.shape
    width_devs = lax.axis_size("wa")
    streams = tokens.transpose(1, 2, 0, 3).reshape(rows_dev * cols_dev, frames, width)
    current = (
        mixer(streams, params_of(0))
        .reshape(rows_dev, cols_dev, frames, width)
        .transpose(2, 0, 1, 3)
    )
    piece = lax.all_to_all(current, "ha", split_axis=0, concat_axis=1, tiled=True)
    frame_part, rows_all, col_count, _ = piece.shape
    streams = piece.transpose(0, 2, 1, 3).reshape(frame_part * col_count, rows_all, width)
    output = mixer(streams, params_of(1))
    current = output.reshape(frame_part, col_count, rows_all, width).transpose(0, 2, 1, 3)
    frame_part = current.shape[0]
    rows_all = current.shape[1]
    split_rows = current.reshape(frame_part, rows_all // width_devs, width_devs, cols_dev, width)
    piece = lax.all_to_all(split_rows, "wa", split_axis=2, concat_axis=3, tiled=True)
    part_frames, row_count, single, cols_all, _ = piece.shape
    streams = piece.reshape(part_frames * row_count * single, cols_all, width)
    output = mixer(streams, params_of(2))
    current = output.reshape(part_frames, row_count, single, cols_all, width)
    returned = one_exchange(current, ("ha", "wa"), ("ha", "wa"), (1, 3), (0, 2))
    result = returned.reshape(frames, rows_dev, cols_dev, width)
    return result


def solution(mesh):
    in_specs = (P("ba", "ha", "wa", None), P(), P(), P(), P(), P(), P(), P(), P(), P(), P(), P())
    out_specs = P("ba", "ha", "wa", None)
    return jax.shard_map(shards, mesh=mesh, in_specs=in_specs, out_specs=out_specs, check_vma=False)
```

profile of v0, /device:TPU:4, one launch (start us, length us, event | category | flops | bytes accessed | tf_op | source)
XLA Modules:
  0.0 170.8 jit_solution(3473395650141608465)
XLA Ops:
  0.6 1.4 fusion.70
  2.0 2.3 %copy_convert_fusion.1 = f32[8,8,8,512]{3,0,2,1:T(8,128)} fusion(bf16[8,8,8,512]{3,2,1,0:T(8,128)(2,1)} %param.12), kind=kLoop, calls=%fused_computation.141 | loop fusion | flops 262144 | bytes 1572864 | tf_op jit(solution)/shard_map/convert_element_type | solution.py:59
  6.1 2.8 %convolution_convert_fusion.2 = bf16[512,2048]{1,0:T(8,128)(2,1)S(1)} fusion(bf16[512,512]{1,0:T(8,128)(2,1)S(1)} %bitcast.272, bf16[3,512,2048]{2,1,0:T(8,128)(2,1)} %param.14), kind=kOutput, calls=%fused_computation.11 | convolution fusion | flops 1074790400 | bytes 4718592 | tf_op jit(solution)/shard_map/dot_general | solution.py:63
  11.7 2.5 %reshape.440 = bf16[64,8,16,64]{3,2,1,0:T(8,128)(2,1)} reshape(bf16[64,8,1024]{2,1,0:T(8,128)(2,1)S(1)} %multiply_convert_fusion.11) | data formatting | bytes 2097152 | tf_op jit(solution)/shard_map/reshape | solution.py:85
  17.5 1.7 %compare_select_fusion = (f32[64,16,8]{1,2,0:T(8,128)}, f32[64,8,16]{2,1,0:T(8,128)S(1)}) fusion(f32[16]{0:T(128)S(1)} %get-tuple-element.39, bf16[64,8,512]{2,1,0:T(8,128)(2,1)S(1)} %bitcast.274, bf16[3,512,16]{1,2,0:T(8,128)(2,1)} %param.16), kind=kOutput, calls=%fused_computation.129 | convolution fusion | flops 8445952 | bytes 606272 | tf_op jit(solution)/shard_map/dot_general | solution.py:65
  21.0 1.4 slice_bitcast_fusion.1
  22.4 3.8 %bitcast_add_fusion.2 = f32[64,8,16,64]{3,1,2,0:T(8,128)S(1)} fusion(bf16[64,8,16,64]{3,2,1,0:T(8,128)(2,1)S(1)} %copy-done.1, f32[16]{0:T(128)S(1)} %get-tuple-element.42, f32[64,16,8]{2,1,0:T(8,128)S(1)} %copy.76, f32[64,16,8]{2,1,0:T(8,128)S(1)} %copy.74, f32[64,8,8]{2,1,0:T(8,128)} %fusion.111, pred[8,8]{1,0:T(8,128)(4,1)} %iota_compare_fusion.1), kind=kOutput, calls=%fused_computation.5 | convolution fusion | flops 10289152 | bytes 3227776 | tf_op jit(solution)/shard_map/nhts,nshp->nthp/dot_general | solution.py:86
  26.2 2.9 %copy.79 = f32[64,8,16,64]{3,2,1,0:T(8,128)} copy(f32[64,8,16,64]{3,1,2,0:T(8,128)S(1)} %bitcast_add_fusion.2) | data formatting | bytes 4194304 | tf_op jit(solution)/shard_map/add | solution.py:87
  29.0 3.5 %reshape.443 = f32[512,1024]{1,0:T(8,128)S(1)} reshape(f32[64,8,16,64]{3,2,1,0:T(8,128)} %copy.79) | data formatting | bytes 4194304 | tf_op jit(solution)/shard_map/reshape | solution.py:88
  32.6 2.1 %multiply_reduce_fusion.2 = f32[512]{0:T(512)S(1)} fusion(f32[512,1024]{1,0:T(8,128)S(1)} %reshape.443, bf16[512,2048]{1,0:T(8,128)(2,1)} %copy-done.4), kind=kLoop, calls=%fused_computation.77 | loop fusion | flops 4193792 | bytes 3147776 | tf_op jit(solution)/shard_map/reduce_sum | solution.py:90
  35.3 2.2 %fusion.55 = bf16[512,512]{1,0:T(8,128)(2,1)S(1)} fusion(f32[512,512]{1,0:T(8,128)S(1)} %bitcast.278, bf16[3,1024,512]{2,1,0:T(8,128)(2,1)} %param.23, f32[1024]{0:T(1024)S(1)} %bitcast.302, f32[512]{0:T(512)S(1)} %add_rsqrt_fusion.5, f32[512,1024]{1,0:T(8,128)S(1)} %reshape.443, bf16[512,2048]{1,0:T(8,128)(2,1)S(1)} %copy-done.5), kind=kOutput, calls=%fused_computation.91 | convolution fusion | flops 542113792 | bytes 5773312 | tf_op jit(solution)/shard_map/dot_general | solution.py:92
  38.4 8.6 %all-to-all-start = ((bf16[8,8,8,512]{3,2,1,0:T(8,128)(2,1)}), bf16[8,8,8,512]{3,2,1,0:T(8,128)(2,1)S(1)}, u32[]{:S(2)}, u32[]{:S(2)}) async-start(bf16[8,8,8,512]{3,2,1,0:T(8,128)(2,1)} %bitcast.261), calls=%async_computation | async-start | bytes 1048576 | tf_op jit(solution)/shard_map/all_to_all | solution.py:135
  47.1 18.0 %all-to-all-done = bf16[8,8,8,512]{3,2,1,0:T(8,128)(2,1)S(1)} async-done(((bf16[8,8,8,512]{3,2,1,0:T(8,128)(2,1)}), bf16[8,8,8,512]{3,2,1,0:T(8,128)(2,1)S(1)}, u32[]{:S(2)}, u32[]{:S(2)}) %all-to-all-start) | async-done | bytes 524320 | tf_op jit(solution)/shard_map/all_to_all | solution.py:135
  66.4 2.9 %convolution_convert_fusion.1 = bf16[512,2048]{1,0:T(8,128)(2,1)S(1)} fusion(bf16[512,512]{1,0:T(8,128)(2,1)S(1)} %bitcast.265, bf16[3,512,2048]{2,1,0:T(8,128)(2,1)} %param.14), kind=kOutput, calls=%fused_computation.10 | convolution fusion | flops 1074790400 | bytes 4718592 | tf_op jit(solution)/shard_map/dot_general | solution.py:63
  69.6 1.6 copy.81
  73.3 1.8 %copy.82 = bf16[8,64,1024]{1,2,0:T(8,128)(2,1)} copy(bf16[8,64,1024]{2,1,0:T(8,128)(2,1)S(1)} %multiply_convert_fusion.9) | data formatting | bytes 2097152 | tf_op jit(solution)/shard_map/convert_element_type | solution.py:70
  76.2 6.3 %reduce-window_bitcast_fusion.1 = f32[8,16,64]{1,0,2:T(8,128)S(1)} fusion(f32[8,64,16]{2,0,1:T(8,128)S(1)} %copy.83), kind=kOutput, calls=%fused_computation.132 | output fusion | flops 516096 | bytes 65536 | tf_op jit(solution)/shard_map/jit(cumsum)/reduce_window_sum | solution.py:77
  82.7 3.7 %bitcast_add_fusion.1 = f32[8,64,16,64]{1,3,2,0:T(8,128)} fusion(bf16[8,64,16,64]{1,3,2,0:T(8,128)(2,1)S(1)} %bitcast.271, f32[16]{0:T(128)S(1)} %copy-done.42, f32[8,16,64]{2,1,0:T(8,128)S(1)} %get-tuple-element.46, f32[8,16,64]{2,1,0:T(8,128)S(1)} %copy.84, f32[8,64,64]{2,1,0:T(8,128)S(1)} %fusion.108, pred[64,64]{1,0:T(8,128)(4,1)S(1)} %iota_compare_fusion), kind=kOutput, calls=%fused_computation.4 | convolution fusion | flops 71303168 | bytes 3346496 | tf_op jit(solution)/shard_map/nhts,nshp->nthp/dot_general | solution.py:86
  86.4 5.7 %copy.86 = f32[8,64,16,64]{3,2,1,0:T(8,128)} copy(f32[8,64,16,64]{1,3,2,0:T(8,128)} %bitcast_add_fusion.1) | data formatting | bytes 4194304 | tf_op jit(solution)/shard_map/add | solution.py:87
  92.1 3.5 %reshape.449 = f32[512,1024]{1,0:T(8,128)S(1)} reshape(f32[8,64,16,64]{3,2,1,0:T(8,128)} %copy.86) | data formatting | bytes 4194304 | tf_op jit(solution)/shard_map/reshape | solution.py:88
  95.6 2.1 %multiply_reduce_fusion.1 = f32[512]{0:T(512)S(1)} fusion(f32[512,1024]{1,0:T(8,128)S(1)} %reshape.449, bf16[512,2048]{1,0:T(8,128)(2,1)} %copy-done.8), kind=kLoop, calls=%fused_computation.67 | loop fusion | flops 4193792 | bytes 3147776 | tf_op jit(solution)/shard_map/reduce_sum | solution.py:90
  97.8 2.2 %fusion.56 = bf16[512,512]{1,0:T(8,128)(2,1)S(1)} fusion(f32[512,512]{1,0:T(8,128)S(1)} %bitcast.280, bf16[3,1024,512]{2,1,0:T(8,128)(2,1)} %param.23, f32[1024]{0:T(1024)S(1)} %bitcast.301, f32[512]{0:T(512)S(1)} %add_rsqrt_fusion.4, f32[512,1024]{1,0:T(8,128)S(1)} %reshape.449, bf16[512,2048]{1,0:T(8,128)(2,1)S(1)} %copy-done.9), kind=kOutput, calls=%fused_computation.92 | convolution fusion | flops 542113792 | bytes 5773312 | tf_op jit(solution)/shard_map/dot_general | solution.py:92
  100.4 14.6 %all_to_all.23 = bf16[1,8,8,8,512]{4,3,1,0,2:T(8,128)(2,1)S(1)} all-to-all(bf16[1,8,8,8,512]{4,3,1,0,2:T(8,128)(2,1)S(1)} %copy.88), channel_id=1, replica_groups=mesh['ha'=8,'wa'=8,'ba'=4] {'wa'}, dimensions={2} | all-to-all | bytes 1048576 | tf_op jit(solution)/shard_map/all_to_all | solution.py:143
  115.4 2.9 %convolution_convert_fusion = bf16[512,2048]{1,0:T(8,128)(2,1)S(1)} fusion(bf16[512,512]{1,0:T(8,128)(2,1)S(1)} %bitcast.263, bf16[3,512,2048]{2,1,0:T(8,128)(2,1)} %param.14), kind=kOutput, calls=%fused_computation.9 | convolution fusion | flops 1074790400 | bytes 4718592 | tf_op jit(solution)/shard_map/dot_general | solution.py:63
  121.3 1.8 %copy.90 = bf16[8,64,1024]{1,2,0:T(8,128)(2,1)} copy(bf16[8,64,1024]{2,1,0:T(8,128)(2,1)S(1)} %multiply_convert_fusion.7) | data formatting | bytes 2097152 | tf_op jit(solution)/shard_map/convert_element_type | solution.py:70
  124.2 6.3 %reduce-window_bitcast_fusion = f32[8,16,64]{1,0,2:T(8,128)S(1)} fusion(f32[8,64,16]{2,0,1:T(8,128)S(1)} %copy.91), kind=kOutput, calls=%fused_computation.131 | output fusion | flops 516096 | bytes 65536 | tf_op jit(solution)/shard_map/jit(cumsum)/reduce_window_sum | solution.py:77
  130.6 3.7 %bitcast_add_fusion = f32[8,64,16,64]{1,3,2,0:T(8,128)} fusion(bf16[8,64,16,64]{1,3,2,0:T(8,128)(2,1)S(1)} %bitcast.270, f32[16]{0:T(128)S(1)} %copy-done.41, f32[8,16,64]{2,1,0:T(8,128)S(1)} %get-tuple-element.48, f32[8,16,64]{2,1,0:T(8,128)S(1)} %copy.92, f32[8,64,64]{2,1,0:T(8,128)S(1)} %fusion.105, pred[64,64]{1,0:T(8,128)(4,1)S(1)} %copy-done.23), kind=kOutput, calls=%fused_computation.3 | convolution fusion | flops 71303168 | bytes 3346496 | tf_op jit(solution)/shard_map/nhts,nshp->nthp/dot_general | solution.py:86
  134.3 5.7 %copy.94 = f32[8,64,16,64]{3,2,1,0:T(8,128)} copy(f32[8,64,16,64]{1,3,2,0:T(8,128)} %bitcast_add_fusion) | data formatting | bytes 4194304 | tf_op jit(solution)/shard_map/add | solution.py:87
  140.0 3.5 %reshape.456 = f32[512,1024]{1,0:T(8,128)S(1)} reshape(f32[8,64,16,64]{3,2,1,0:T(8,128)} %copy.94) | data formatting | bytes 4194304 | tf_op jit(solution)/shard_map/reshape | solution.py:88
  143.6 2.1 %multiply_reduce_fusion = f32[512]{0:T(512)S(1)} fusion(f32[512,1024]{1,0:T(8,128)S(1)} %reshape.456, bf16[512,2048]{1,0:T(8,128)(2,1)} %copy-done.6), kind=kLoop, calls=%fused_computation.59 | loop fusion | flops 4193792 | bytes 3147776 | tf_op jit(solution)/shard_map/reduce_sum | solution.py:90
  145.8 2.2 %fusion.58 = bf16[64,1,1,1,8,512]{5,4,3,2,1,0:T(8,128)(2,1)S(1)} fusion(f32[512,512]{1,0:T(8,128)S(1)} %bitcast.279, bf16[3,1024,512]{2,1,0:T(8,128)(2,1)} %param.23, f32[1024]{0:T(1024)S(1)} %bitcast.300, f32[512]{0:T(512)S(1)} %add_rsqrt_fusion.3, f32[512,1024]{1,0:T(8,128)S(1)} %reshape.456, bf16[512,2048]{1,0:T(8,128)(2,1)S(1)} %copy-done.7), kind=kOutput, calls=%fused_computation.94 | convolution fusion | flops 542113792 | bytes 5773312 | tf_op jit(solution)/shard_map/dot_general | solution.py:92
  148.0 22.0 %all_to_all.24 = bf16[64,1,1,1,8,512]{5,4,3,2,1,0:T(8,128)(2,1)S(1)} all-to-all(bf16[64,1,1,1,8,512]{5,4,3,2,1,0:T(8,128)(2,1)S(1)} %fusion.58), channel_id=1, replica_groups=mesh['ha'=8,'wa'=8,'ba'=4] {'ha','wa'}, dimensions={0} | all-to-all | bytes 1048576 | tf_op jit(solution)/shard_map/all_to_all | solution.py:25
  (142 shorter events, 22.4 us)
Async XLA Ops:
  0.0 5.5 %copy-start = (bf16[8,8,8,512]{3,2,1,0:T(8,128)(2,1)S(1)}, bf16[8,8,8,512]{3,2,1,0:T(8,128)(2,1)}, u32[]{:S(2)}) copy-start(bf16[8,8,8,512]{3,2,1,0:T(8,128)(2,1)} %param.12) | copy-start | bytes 1572868
  0.0 4.3 %copy-start.13 = (f32[3,4,1024]{2,1,0:T(4,128)S(1)}, f32[3,4,1024]{2,1,0:T(4,128)}, u32[]{:S(2)}) copy-start(f32[3,4,1024]{2,1,0:T(4,128)} %param.17) | copy-start | bytes 147460
  0.0 4.9 %copy-start.25 = (f32[3,512]{1,0:T(4,128)S(1)}, f32[3,512]{1,0:T(4,128)}, u32[]{:S(2)}) copy-start(f32[3,512]{1,0:T(4,128)} %param.13) | copy-start | bytes 18436
  11.6 2.5 %copy-start.24 = (f32[3,4,128]{2,1,0:T(4,128)S(1)}, f32[3,4,128]{2,1,0:T(4,128)}, u32[]{:S(2)}) copy-start(f32[3,4,128]{2,1,0:T(4,128)} %param.18) | copy-start | bytes 18436
  11.6 3.1 %copy-start.12 = (bf16[3,512,128]{2,1,0:T(8,128)(2,1)S(1)}, bf16[3,512,128]{2,1,0:T(8,128)(2,1)}, u32[]{:S(2)}) copy-start(bf16[3,512,128]{2,1,0:T(8,128)(2,1)} %param.15) | copy-start | bytes 1179652
  11.6 4.6 %copy-start.39 = (f32[3,16]{1,0:T(4,128)S(1)}, f32[3,16]{1,0:T(4,128)}, u32[]{:S(2)}) copy-start(f32[3,16]{1,0:T(4,128)} %param.19) | copy-start | bytes 580
  11.7 5.2 %copy-start.40 = (f32[3,16]{1,0:T(4,128)S(1)}, f32[3,16]{1,0:T(4,128)}, u32[]{:S(2)}) copy-start(f32[3,16]{1,0:T(4,128)} %param.20) | copy-start | bytes 580
  15.3 7.1 %copy-start.1 = (bf16[64,8,16,64]{3,2,1,0:T(8,128)(2,1)S(1)}, bf16[64,8,16,64]{3,2,1,0:T(8,128)(2,1)}, u32[]{:S(2)}) copy-start(bf16[64,8,16,64]{3,2,1,0:T(8,128)(2,1)} %reshape.440) | copy-start | bytes 3145732
  29.0 5.6 %copy-start.19 = (f32[3,1024]{1,0:T(4,128)S(1)}, f32[3,1024]{1,0:T(4,128)}, u32[]{:S(2)}) copy-start(f32[3,1024]{1,0:T(4,128)} %param.22) | copy-start | bytes 36868
  32.5 2.7 %copy-start.5 = (bf16[512,2048]{1,0:T(8,128)(2,1)S(1)}, bf16[512,2048]{1,0:T(8,128)(2,1)}, u32[]{:S(2)}) copy-start(bf16[512,2048]{1,0:T(8,128)(2,1)} %copy-done.4) | copy-start | bytes 6291460
  32.5 2.7 %copy-start.10 = (f32[8,8,8,512]{3,0,2,1:T(8,128)S(1)}, f32[8,8,8,512]{3,0,2,1:T(8,128)}, u32[]{:S(2)}) copy-start(f32[8,8,8,512]{3,0,2,1:T(8,128)} %copy_convert_fusion.1) | copy-start | bytes 3145732
  38.4 27.4 %copy-start.21 = (f32[1,512]{1,0:T(1,128)S(1)}, f32[1,512]{1,0:T(1,128)}, u32[]{:S(2)}) copy-start(f32[1,512]{1,0:T(1,128)} %get-tuple-element.22) | copy-start | bytes 6148
  38.4 26.6 %all-to-all-start = ((bf16[8,8,8,512]{3,2,1,0:T(8,128)(2,1)}), bf16[8,8,8,512]{3,2,1,0:T(8,128)(2,1)S(1)}, u32[]{:S(2)}, u32[]{:S(2)}) async-start(bf16[8,8,8,512]{3,2,1,0:T(8,128)(2,1)} %bitcast.261), calls=%async_computation | async-start | bytes 1048576 | tf_op jit(solution)/shard_map/all_to_all | solution.py:135
  47.1 35.6 %copy-start.22 = (pred[64,64]{1,0:T(8,128)(4,1)}, pred[64,64]{1,0:T(8,128)(4,1)S(1)}, u32[]{:S(2)}) copy-start(pred[64,64]{1,0:T(8,128)(4,1)S(1)} %iota_compare_fusion) | copy-start | bytes 12292
  69.3 2.0 %copy-start.8 = (bf16[512,2048]{1,0:T(8,128)(2,1)}, bf16[512,2048]{1,0:T(8,128)(2,1)S(1)}, u32[]{:S(2)}) copy-start(bf16[512,2048]{1,0:T(8,128)(2,1)S(1)} %convolution_convert_fusion.1) | copy-start | bytes 6291460
  73.3 1.9 %copy-start.31 = (f32[128]{0:T(128)S(1)}, f32[128]{0:T(128)}, u32[]{:S(2)}) copy-start(f32[128]{0:T(128)} %get-tuple-element.25) | copy-start | bytes 1540
  73.3 1.9 %copy-start.32 = (f32[128]{0:T(128)S(1)}, f32[128]{0:T(128)}, u32[]{:S(2)}) copy-start(f32[128]{0:T(128)} %get-tuple-element.26) | copy-start | bytes 1540
  73.3 2.3 %copy-start.14 = (bf16[3,512,16]{1,2,0:T(8,128)(2,1)S(1)}, bf16[3,512,16]{1,2,0:T(8,128)(2,1)}, u32[]{:S(2)}) copy-start(bf16[3,512,16]{1,2,0:T(8,128)(2,1)} %param.16) | copy-start | bytes 147460
  73.3 2.3 %copy-start.37 = (f32[16]{0:T(128)S(1)}, f32[16]{0:T(128)}, u32[]{:S(2)}) copy-start(f32[16]{0:T(128)} %get-tuple-element.40) | copy-start | bytes 196
  73.3 2.7 %copy-start.38 = (f32[16]{0:T(128)S(1)}, f32[16]{0:T(128)}, u32[]{:S(2)}) copy-start(f32[16]{0:T(128)} %get-tuple-element.37) | copy-start | bytes 196
  75.1 7.6 %copy-start.3 = (bf16[8,64,1024]{1,2,0:T(8,128)(2,1)S(1)}, bf16[8,64,1024]{1,2,0:T(8,128)(2,1)}, u32[]{:S(2)}) copy-start(bf16[8,64,1024]{1,2,0:T(8,128)(2,1)} %copy.82) | copy-start | bytes 3145732
  75.1 7.6 %copy-start.42 = (f32[16]{0:T(128)S(1)}, f32[16]{0:T(128)}, u32[]{:S(2)}) copy-start(f32[16]{0:T(128)} %get-tuple-element.43) | copy-start | bytes 196
  95.6 2.1 %copy-start.9 = (bf16[512,2048]{1,0:T(8,128)(2,1)S(1)}, bf16[512,2048]{1,0:T(8,128)(2,1)}, u32[]{:S(2)}) copy-start(bf16[512,2048]{1,0:T(8,128)(2,1)} %copy-done.8) | copy-start | bytes 6291460
  95.6 2.2 %copy-start.11 = (f32[1,64,8,512]{3,1,2,0:T(8,128)S(1)}, f32[1,64,8,512]{3,1,2,0:T(8,128)}, u32[]{:S(2)}) copy-start(f32[1,64,8,512]{3,1,2,0:T(8,128)} %copy.81) | copy-start | bytes 3145732
  100.0 15.2 %copy-start.20 = (f32[1,512]{1,0:T(1,128)S(1)}, f32[1,512]{1,0:T(1,128)}, u32[]{:S(2)}) copy-start(f32[1,512]{1,0:T(1,128)} %get-tuple-element.20) | copy-start | bytes 6148
  121.3 2.3 %copy-start.35 = (f32[16]{0:T(128)S(1)}, f32[16]{0:T(128)}, u32[]{:S(2)}) copy-start(f32[16]{0:T(128)} %get-tuple-element.38) | copy-start | bytes 196
  121.3 2.6 %copy-start.36 = (f32[16]{0:T(128)S(1)}, f32[16]{0:T(128)}, u32[]{:S(2)}) copy-start(f32[16]{0:T(128)} %get-tuple-element.35) | copy-start | bytes 196
  123.1 7.6 %copy-start.2 = (bf16[8,64,1024]{1,2,0:T(8,128)(2,1)S(1)}, bf16[8,64,1024]{1,2,0:T(8,128)(2,1)}, u32[]{:S(2)}) copy-start(bf16[8,64,1024]{1,2,0:T(8,128)(2,1)} %copy.90) | copy-start | bytes 3145732
  123.1 7.6 %copy-start.23 = (pred[64,64]{1,0:T(8,128)(4,1)S(1)}, pred[64,64]{1,0:T(8,128)(4,1)}, u32[]{:S(2)}) copy-start(pred[64,64]{1,0:T(8,128)(4,1)} %copy-done.22) | copy-start | bytes 12292
  123.1 7.6 %copy-start.41 = (f32[16]{0:T(128)S(1)}, f32[16]{0:T(128)}, u32[]{:S(2)}) copy-start(f32[16]{0:T(128)} %get-tuple-element.41) | copy-start | bytes 196
  143.5 2.2 %copy-start.7 = (bf16[512,2048]{1,0:T(8,128)(2,1)S(1)}, bf16[512,2048]{1,0:T(8,128)(2,1)}, u32[]{:S(2)}) copy-start(bf16[512,2048]{1,0:T(8,128)(2,1)} %copy-done.6) | copy-start | bytes 6291460
  143.5 2.2 %copy-start.26 = (f32[1,1024]{1,0:T(1,128)S(1)}, f32[1,1024]{1,0:T(1,128)}, u32[]{:S(2)}) copy-start(f32[1,1024]{1,0:T(1,128)} %get-tuple-element.17) | copy-start | bytes 12292
  (12 other events, 17.0 us)
where the time goes:
time: 172 us; the launch traced here: 171 us
  local copies, waits for them, and re-layouts  42.8 us (25%)
  blocking collectives  36.6 us (21%)
  matrix products  32.1 us (19%)
  other arithmetic  31.9 us (19%)
  waiting for transfers between devices  18 us (10%)
  starting transfers between devices  8.6 us (5%)
    all_to_all x1, blocking collectives, one_exchange(): tiles = lax.all_to_all(tiles, axis, split_axis=0, concat_axis=0, tiled=True)  22 us
    all_to_all x1, waiting for transfers between devices, shards(): lax.all_to_all(current, 'ha', split_axis=0, concat_axis=1, tiled=True)  18 us
    all_to_all x1, blocking collectives, shards(): lax.all_to_all(split_rows, 'wa', split_axis=2, concat_axis=3, tiled=True)  14.6 us
    add x3, local copies, waits for them, and re-layouts, mixer(): mixed = mixed + skip_gain[:, None] * heads_in.astype(jnp.float32)  14.3 us
    another operation x3, other arithmetic, mixer(): cumul = jnp.cumsum(steps * -jnp.exp(rate_log), axis=1).transpose(0, 2, 1)  12.9 us
    dot_general x3, matrix products, mixer(): jnp.einsum('nhts,nshp->nthp', weights, heads_in, preferred_element_type=j...  11.1 us
    reshape x3, local copies, waits for them, and re-layouts, mixer(): mixed.reshape(count * length, inner) * jax.nn.silu(gate.astype(jnp.float32))  10.5 us
    all_to_all x1, starting transfers between devices, shards(): lax.all_to_all(current, 'ha', split_axis=0, concat_axis=1, tiled=True)  8.6 us
  transfers between devices with their start and end apart: 1, of which 1 were waited for; matrix products, arithmetic and copies ran while one was open for 0% of the time, Pallas kernels for 0%

commit v1 on v0

v1 whole, which is shorter than its diff:
```python
import functools

import jax
import jax.numpy as jnp
from jax import lax
from jax.experimental import pallas as pl
from jax.experimental.pallas import tpu as pltpu
from jax.sharding import PartitionSpec as P

LINES = 8
LENGTH = 64
ROWS = LINES * LENGTH
WIDTH = 512
INNER = 1024
HEADS = 16
STATES = 64
STEPS = 4
CHUNK = INNER // STEPS
LANES = 128
LOG2E = 1.4426950408889634
F32 = jnp.float32
BF16 = jnp.bfloat16


def iota(shape, dim):
    return lax.broadcasted_iota(jnp.int32, shape, dim)


def dot(a, b):
    return jnp.dot(a, b, preferred_element_type=F32)


def dot_t(a, b):
    return lax.dot_general(a, b, (((1,), (1,)), ((), ())), preferred_element_type=F32)


def split3(value):
    high = value.astype(BF16)
    rest = value - high.astype(F32)
    middle = rest.astype(BF16)
    low = (rest - middle.astype(F32)).astype(BF16)
    return high, middle, low


def swap_matrix():
    r, c = iota((64, 64), 0), iota((64, 64), 1)
    return ((r // 8 == c % 8) & (r % 8 == c // 8)).astype(BF16)


def half_silu(half):
    return half + half * jnp.tanh(half)


def kernel(
    layer,
    stride,
    x_ref,
    norm_ref,
    wgate_ref,
    wvalue_ref,
    wcoup_ref,
    wsteps_ref,
    taps_ref,
    ctaps_ref,
    bias_ref,
    rate_ref,
    skip_ref,
    ogain_ref,
    wout_hbm,
    out_ref,
    xf,
    normed,
    padded,
    cpadded,
    scores,
    cum,
    rowside,
    skipx,
    gates,
    gated,
    sumsq,
    wout,
    sem,
):
    j = pl.program_id(0)
    pad = 8 if stride == 1 else 24
    span = LENGTH + pad

    row = iota((LENGTH, LANES), 0)
    col = iota((LENGTH, LANES), 1) % LENGTH
    if stride == 1:
        keep = col <= row
    else:
        keep = (col // stride <= row // stride) & (col % stride == row % stride)

    def load_line(s):
        if layer == 0:
            return xf[:, s * 8 : (s + 1) * 8, :].reshape(LENGTH, WIDTH)
        return x_ref[:, s].astype(F32).reshape(LENGTH, WIDTH)

    copy = pltpu.make_async_copy(wout_hbm.at[layer], wout, sem)

    @pl.when(j == 0)
    def _():
        copy.start()
        if layer == 0:
            swap = swap_matrix()
            for f in range(8):
                xf[f] = dot(swap, x_ref[f].astype(F32).reshape(64, WIDTH).astype(BF16))
        gain = norm_ref[layer : layer + 1, :]
        for s in range(LINES):
            x = load_line(s)
            scale = lax.rsqrt(jnp.mean(x * x, axis=-1, keepdims=True) + 1e-05)
            normed[s * LENGTH : (s + 1) * LENGTH, :] = (x * scale * gain).astype(BF16)

        copies = (iota((LANES, HEADS), 0) % HEADS == iota((LANES, HEADS), 1)).astype(BF16)
        wsteps = dot(copies, wsteps_ref[...]).astype(BF16)
        coupling = dot(normed[...], wcoup_ref[...])
        steps_raw = dot_t(normed[...], wsteps)

        padded[...] = jnp.zeros_like(padded)
        cpadded[...] = jnp.zeros_like(cpadded)
        taps = ctaps_ref[...] * 0.5
        for s in range(LINES):
            cpadded[s * span + pad : (s + 1) * span, :] = coupling[s * LENGTH : (s + 1) * LENGTH, :]
        bias = jnp.concatenate([bias_ref[layer : layer + 1, :]] * 8, axis=1)
        rate = jnp.concatenate([-jnp.exp(rate_ref[layer : layer + 1, :]) * LOG2E] * 8, axis=1)
        tri = keep[:, :LENGTH].astype(BF16)
        tri3 = jnp.concatenate([tri] * 3, axis=1)
        lane = iota((LENGTH, LANES), 1)
        for s in range(LINES):
            base = s * span + pad
            half = sum(
                cpadded[base - (3 - k) * stride : base - (3 - k) * stride + LENGTH, :] * taps[k : k + 1, :]
                for k in range(4)
            )
            maps = half_silu(half)
            inputs = maps[:, :STATES].astype(BF16)
            outputs = maps[:, STATES:].astype(BF16)
            scores[s] = dot_t(outputs, jnp.concatenate([inputs, inputs], axis=0))

            raw = steps_raw[s * LENGTH : (s + 1) * LENGTH, :] + bias
            e = jnp.exp(-jnp.abs(raw))
            steps = jnp.maximum(raw, 0.0) + jnp.where(e < 1e-3, e - 0.5 * e * e, jnp.log(1.0 + e))
            total = dot(tri3, jnp.concatenate(split3(steps * rate), axis=0))
            high, middle, low = split3(total)
            cum[s * LENGTH : (s + 1) * LENGTH, :] = jnp.where(
                lane < HEADS, high, jnp.where(lane < 2 * HEADS, middle, low)
            )
            side = total - jnp.log(steps) * LOG2E
            rowside[s] = jnp.transpose(jnp.concatenate([side, side], axis=0))[:HEADS, :]

        spread = (iota((HEADS, INNER), 1) // STATES == iota((HEADS, INNER), 0)).astype(F32)
        skip = jnp.dot(
            jnp.broadcast_to(skip_ref[layer : layer + 1, :], (8, HEADS)),
            spread,
            precision=lax.Precision.HIGHEST,
            preferred_element_type=F32,
        )
        for c in range(STEPS):
            skipx[c] = skip[:, c * CHUNK : (c + 1) * CHUNK]
        sumsq[...] = jnp.zeros_like(sumsq)

    lane3 = iota((LANES, CHUNK), 0)
    expand = (
        (lane3 < 3 * HEADS) & (lane3 % HEADS == 4 * j + iota((LANES, CHUNK), 1) // STATES)
    ).astype(BF16)
    taps = taps_ref[...] * 0.5
    lower = iota((LENGTH, LANES), 1) < STATES
    lower1 = iota((1, LANES), 1) < STATES
    zero = jnp.zeros((LENGTH, LANES), BF16)
    for b in range(2):
        rows = slice(b * 256, (b + 1) * 256)
        value = dot(normed[rows, :], wvalue_ref[...])
        for q in range(4):
            s = b * 4 + q
            for t in range(2):
                padded[t, s * span + pad : (s + 1) * span, :] = value[
                    q * LENGTH : (q + 1) * LENGTH, t * LANES : (t + 1) * LANES
                ]
        gates[rows, :] = half_silu(dot(normed[rows, :], wgate_ref[...]) * 0.5)
        time_side = dot(cum[rows, :], expand)
        for q in range(4):
            s = b * 4 + q
            here = slice(s * LENGTH, (s + 1) * LENGTH)
            base = s * span + pad
            square = sumsq[here, :]
            for t in range(2):
                lanes = slice(t * LANES, (t + 1) * LANES)
                half = sum(
                    padded[t, base - (3 - k) * stride : base - (3 - k) * stride + LENGTH, :] * taps[k : k + 1, lanes]
                    for k in range(4)
                )
                xs = half_silu(half).astype(BF16)
                head = 4 * j + 2 * t
                side = jnp.where(lower1, rowside[s, pl.ds(head, 1), :], rowside[s, pl.ds(head + 1, 1), :])
                power = jnp.where(keep, time_side[q * LENGTH : (q + 1) * LENGTH, lanes] - side, -jnp.inf)
                weights = (scores[s] * jnp.exp2(power)).astype(BF16)
                pair = jnp.concatenate([jnp.where(lower, xs, zero), jnp.where(lower, zero, xs)], axis=0)
                mixed = dot(weights, pair) + skipx[j, 0:1, lanes] * xs.astype(F32)
                mixed = mixed * gates[here, lanes]
                square = square + mixed * mixed
                gated[j, here, lanes] = (mixed * ogain_ref[layer : layer + 1, lanes]).astype(BF16)
            sumsq[here, :] = square

    @pl.when(j == STEPS - 1)
    def _():
        copy.wait()
        for b in range(2):
            rows = slice(b * 256, (b + 1) * 256)
            update = dot(gated[0, rows, :], wout[0:CHUNK, :])
            for c in range(1, STEPS):
                update = update + dot(gated[c, rows, :], wout[c * CHUNK : (c + 1) * CHUNK, :])
            scale = lax.rsqrt(jnp.sum(sumsq[rows, :], axis=-1, keepdims=True) * (1.0 / INNER) + 1e-05)
            update = update * scale
            for q in range(4):
                s = b * 4 + q
                y = load_line(s) + update[q * LENGTH : (q + 1) * LENGTH, :]
                if layer == 0:
                    out_ref[:, s] = y.reshape(8, 8, WIDTH).astype(BF16)
                elif layer == 1:
                    xf[:, s * 8 : (s + 1) * 8, :] = y.reshape(8, 8, WIDTH)
                else:
                    out_ref[s] = y.reshape(8, 8, WIDTH).astype(BF16)
        if layer == 1:
            swap = swap_matrix()
            for i in range(8):
                turned = dot(swap, xf[i].astype(BF16))
                out_ref[:, i] = turned.reshape(8, 8, WIDTH).astype(BF16)


def mixer(x, layer, params):
    stride = 8 if layer == 0 else 1
    pad = 8 if stride == 1 else 24
    span = LENGTH + pad

    def whole(shape):
        return pl.BlockSpec(shape, lambda j: (0,) * len(shape))

    in_specs = [
        whole((8, 8, 8, WIDTH)),
        whole((3, WIDTH)),
        pl.BlockSpec((None, WIDTH, CHUNK), lambda j: (layer, 0, j)),
        pl.BlockSpec((None, WIDTH, CHUNK), lambda j: (layer, 0, STEPS + j)),
        pl.BlockSpec((None, WIDTH, 2 * STATES), lambda j: (layer, 0, 0)),
        pl.BlockSpec((None, HEADS, WIDTH), lambda j: (layer, 0, 0)),
        pl.BlockSpec((None, 4, CHUNK), lambda j: (layer, 0, j)),
        pl.BlockSpec((None, 4, 2 * STATES), lambda j: (layer, 0, 0)),
        whole((3, HEADS)),
        whole((3, HEADS)),
        whole((3, HEADS)),
        pl.BlockSpec((3, CHUNK), lambda j: (0, j)),
        pl.BlockSpec(memory_space=pl.ANY),
    ]
    scratch = [
        pltpu.VMEM((8, 64, WIDTH), F32),
        pltpu.VMEM((ROWS, WIDTH), BF16),
        pltpu.VMEM((2, LINES * span, LANES), F32),
        pltpu.VMEM((LINES * span, LANES), F32),
        pltpu.VMEM((LINES, LENGTH, LANES), F32),
        pltpu.VMEM((ROWS, LANES), BF16),
        pltpu.VMEM((LINES, HEADS, LANES), F32),
        pltpu.VMEM((STEPS, 8, CHUNK), F32),
        pltpu.VMEM((ROWS, CHUNK), F32),
        pltpu.VMEM((STEPS, ROWS, CHUNK), BF16),
        pltpu.VMEM((ROWS, LANES), F32),
        pltpu.VMEM((INNER, WIDTH), BF16),
        pltpu.SemaphoreType.DMA,
    ]
    if layer == 0:
        x, *params = (pltpu.with_memory_space_constraint(p, pltpu.HBM) for p in (x, *params))
    (norm_gain, w_gatevals, w_coupling, w_steps, conv_values, conv_coupling,
     step_bias, rate_log, skip_gain, out_gain, w_output) = params
    return pl.pallas_call(
        functools.partial(kernel, layer, stride),
        grid=(STEPS,),
        in_specs=in_specs,
        out_specs=whole((8, 8, 8, WIDTH)),
        out_shape=jax.ShapeDtypeStruct((8, 8, 8, WIDTH), BF16),
        scratch_shapes=scratch,
        name=f"mixer{layer}",
        compiler_params=pltpu.CompilerParams(dimension_semantics=("arbitrary",), vmem_limit_bytes=24 * 2**20),
        cost_estimate=pl.CostEstimate(flops=2_000_000_000, bytes_accessed=5_000_000, transcendentals=2_000_000),
    )(x, norm_gain, w_gatevals, w_gatevals, w_coupling, w_steps, conv_values, conv_coupling,
      step_bias, rate_log, skip_gain, out_gain, w_output)


def shards(tokens, *params):
    params = params[:3] + (jnp.swapaxes(params[3], 1, 2),) + params[4:]
    current = mixer(tokens, 0, params)
    current = lax.all_to_all(current, "ha", split_axis=0, concat_axis=0, tiled=True)
    current = mixer(current, 1, params)
    current = lax.all_to_all(current, "wa", split_axis=0, concat_axis=0, tiled=True)
    current = mixer(current, 2, params)
    current = current.reshape(64, 8, WIDTH)
    current = lax.all_to_all(current, ("ha", "wa"), split_axis=0, concat_axis=0, tiled=True)
    return current.reshape(8, 8, 8, WIDTH)


def solution(mesh):
    spec = P("ba", "ha", "wa", None)
    return jax.shard_map(shards, mesh=mesh, in_specs=(spec,) + (P(),) * 11, out_specs=spec, check_vma=False)
```

time: 172 us -> 83.4 us (0.48)
  local copies, waits for them, and re-layouts: 42.8 us -> 0.84 us
  matrix products: 32.1 us -> 0 us
  other arithmetic: 31.9 us -> 0 us
  blocking collectives: 36.6 us -> 62 us
  Pallas kernels: 0 us -> 19.9 us
  waiting for transfers between devices: 18 us -> 0 us
  starting transfers between devices: 8.6 us -> 0 us
    dot_general x18 -> x0, matrix products: 32.1 us -> none  [the longest x3 11.1 us: mixer(): jnp.einsum('nhts,nshp->nthp', weights, heads_in, preferred_element_type=j...]
    all_to_all x2 -> x3, blocking collectives: 36.6 us -> 62 us  [the longest x1 26.3 us: shards(): lax.all_to_all(current, 'ha', split_axis=0, concat_axis=0, tiled=True)]
    pallas_call x0 -> x3, Pallas kernels: none -> 19.9 us  [mixer(): pl.pallas_call(functools.partial(kernel, layer, stride), grid=(STEPS,), i...]
    all_to_all x1 -> x0, waiting for transfers between devices: 18 us -> none  [shards(): lax.all_to_all(current, 'ha', split_axis=0, concat_axis=1, tiled=True)]
    add x4 -> x0, local copies, waits for them, and re-layouts: 14.9 us -> none  [the longest x3 14.3 us: mixer(): mixed = mixed + skip_gain[:, None] * heads_in.astype(jnp.float32)]
    reshape x5 -> x0, local copies, waits for them, and re-layouts: 13 us -> none  [the longest x3 10.5 us: mixer(): mixed.reshape(count * length, inner) * jax.nn.silu(gate.astype(jnp.float32))]
    another operation x3 -> x0, other arithmetic: 12.9 us -> none  [mixer(): cumul = jnp.cumsum(steps * -jnp.exp(rate_log), axis=1).transpose(0, 2, 1)]
    all_to_all x1 -> x0, starting transfers between devices: 8.6 us -> none  [shards(): lax.all_to_all(current, 'ha', split_axis=0, concat_axis=1, tiled=True)]
  transfers between devices with their start and end apart: 1 -> 0, of which waited for: 1 -> 0; matrix products, arithmetic and copies ran while one was open for 0% -> 0% of each run, Pallas kernels for 0% -> 0%
where the time goes in v1:
time: 83.4 us; the launch traced here: 82.8 us
  blocking collectives  62 us (74%)
  Pallas kernels  19.9 us (24%)
  local copies, waits for them, and re-layouts  0.84 us (1%)
    all_to_all x1, blocking collectives, shards(): lax.all_to_all(current, 'ha', split_axis=0, concat_axis=0, tiled=True)  26.3 us
    all_to_all x1, blocking collectives, shards(): lax.all_to_all(current, ('ha', 'wa'), split_axis=0, concat_axis=0, tiled=...  22.8 us
    pallas_call x3, Pallas kernels, mixer(): pl.pallas_call(functools.partial(kernel, layer, stride), grid=(STEPS,), i...  19.9 us
    all_to_all x1, blocking collectives, shards(): lax.all_to_all(current, 'wa', split_axis=0, concat_axis=0, tiled=True)  13 us

profile of v1, /device:TPU:4, one launch (start us, length us, event | category | flops | bytes accessed | tf_op | source)
XLA Modules:
  0.0 82.8 jit_solution(5991430650454593389)
XLA Ops:
  0.0 0.0 copy-start
  0.0 0.0 copy-start.1
  0.0 0.0 copy-start.2
  0.0 0.0 copy-start.3
  0.0 0.0 copy-start.4
  0.0 0.0 copy-start.5
  0.0 0.0 copy-start.6
  0.0 0.0 copy-start.7
  0.1 0.0 copy-start.8
  0.1 0.0 copy-start.9
  0.1 0.0 copy-start.10
  0.1 7.5 %mixer0.1 = bf16[8,8,8,512]{3,2,1,0:T(8,128)(2,1)S(1)} custom-call(bf16[8,8,8,512]{3,2,1,0:T(8,128)(2,1)} %x_ref.1, f32[3,512]{1,0:T(4,128)} %norm_ref.5, bf16[3,512,2048]{2,1,0:T(8,128)(2,1)} %wvalue_ref.5, bf16[3,512,2048]{2,1,0:T(8,128)(2,1)} %wvalue_ref.5, bf16[3,512,128]{2,1,0:T(8,128)(2,1)} %wcoup_ref.5, bf16[3,16,512]{2,1,0:T(8,128)(2,1)} %bitcast.4, ...), custom_call_target="tpu_custom_call" | custom-call | flops 2000000000 | bytes 5000000 | tf_op jit(solution)/shard_map/mixer0/pallas_call | solution.py:274
  7.6 26.3 %all_to_all.15.x_ref = bf16[8,8,8,512]{3,2,1,0:T(8,128)(2,1)S(1)} all-to-all(bf16[8,8,8,512]{3,2,1,0:T(8,128)(2,1)S(1)} %mixer0.1), channel_id=1, replica_groups=mesh['ha'=8,'wa'=8,'ba'=4] {'ha'}, dimensions={0} | all-to-all | bytes 1048576 | tf_op jit(solution)/shard_map/all_to_all | solution.py:291
  33.8 0.0 copy-done
  33.8 0.0 copy-done.1
  33.8 0.0 copy-done.2
  33.8 0.0 copy-done.3
  33.8 0.0 copy-done.4
  33.9 0.0 copy-done.5
  33.9 0.0 copy-done.6
  33.9 0.0 copy-done.7
  33.9 0.0 copy-done.8
  33.9 0.0 copy-done.9
  33.9 0.0 copy-done.10
  33.9 6.4 %mixer1.1 = bf16[8,8,8,512]{3,2,1,0:T(8,128)(2,1)S(1)} custom-call(bf16[8,8,8,512]{3,2,1,0:T(8,128)(2,1)S(1)} %all_to_all.15.x_ref, f32[3,512]{1,0:T(4,128)S(1)} %copy-done.6, bf16[3,512,2048]{2,1,0:T(8,128)(2,1)S(1)} %copy-done, bf16[3,512,2048]{2,1,0:T(8,128)(2,1)S(1)} %copy-done, bf16[3,512,128]{2,1,0:T(8,128)(2,1)S(1)} %copy-done.2, ...), custom_call_target="tpu_custom_call" | custom-call | flops 2000000000 | bytes 5000000 | tf_op jit(solution)/shard_map/mixer1/pallas_call | solution.py:274
  40.3 13.0 %all_to_all.16.x_ref = bf16[8,8,8,512]{3,2,1,0:T(8,128)(2,1)S(1)} all-to-all(bf16[8,8,8,512]{3,2,1,0:T(8,128)(2,1)S(1)} %mixer1.1), channel_id=1, replica_groups=mesh['ha'=8,'wa'=8,'ba'=4] {'wa'}, dimensions={0} | all-to-all | bytes 1048576 | tf_op jit(solution)/shard_map/all_to_all | solution.py:293
  53.2 6.1 %mixer2.1 = bf16[8,8,8,512]{3,2,1,0:T(8,128)(2,1)S(1)} custom-call(bf16[8,8,8,512]{3,2,1,0:T(8,128)(2,1)S(1)} %all_to_all.16.x_ref, f32[3,512]{1,0:T(4,128)S(1)} %copy-done.6, bf16[3,512,2048]{2,1,0:T(8,128)(2,1)S(1)} %copy-done, bf16[3,512,2048]{2,1,0:T(8,128)(2,1)S(1)} %copy-done, bf16[3,512,128]{2,1,0:T(8,128)(2,1)S(1)} %copy-done.2, ...), custom_call_target="tpu_custom_call" | custom-call | flops 2000000000 | bytes 5000000 | tf_op jit(solution)/shard_map/mixer2/pallas_call | solution.py:274
  59.3 22.8 %all_to_all.17 = bf16[64,8,512]{2,1,0:T(8,128)(2,1)S(1)} all-to-all(bf16[64,8,512]{2,1,0:T(8,128)(2,1)S(1)} %bitcast.3), channel_id=1, replica_groups=mesh['ha'=8,'wa'=8,'ba'=4] {'ha','wa'}, dimensions={0} | all-to-all | bytes 1048576 | tf_op jit(solution)/shard_map/all_to_all | solution.py:296
  82.1 0.8 copy.14
Async XLA Ops:
  0.0 33.8 %copy-start = (bf16[3,512,2048]{2,1,0:T(8,128)(2,1)S(1)}, bf16[3,512,2048]{2,1,0:T(8,128)(2,1)}, u32[]{:S(2)}) copy-start(bf16[3,512,2048]{2,1,0:T(8,128)(2,1)} %wvalue_ref.5) | copy-start | bytes 18874372
  0.0 33.8 %copy-start.1 = (bf16[3,1024,512]{2,1,0:T(8,128)(2,1)S(1)}, bf16[3,1024,512]{2,1,0:T(8,128)(2,1)}, u32[]{:S(2)}) copy-start(bf16[3,1024,512]{2,1,0:T(8,128)(2,1)} %wout_hbm.5) | copy-start | bytes 9437188
  0.0 33.8 %copy-start.2 = (bf16[3,512,128]{2,1,0:T(8,128)(2,1)S(1)}, bf16[3,512,128]{2,1,0:T(8,128)(2,1)}, u32[]{:S(2)}) copy-start(bf16[3,512,128]{2,1,0:T(8,128)(2,1)} %wcoup_ref.5) | copy-start | bytes 1179652
  0.0 33.8 %copy-start.3 = (bf16[3,512,16]{1,2,0:T(8,128)(2,1)S(1)}, bf16[3,512,16]{1,2,0:T(8,128)(2,1)}, u32[]{:S(2)}) copy-start(bf16[3,512,16]{1,2,0:T(8,128)(2,1)} %param.16) | copy-start | bytes 147460
  0.0 33.8 %copy-start.4 = (f32[3,4,1024]{2,1,0:T(4,128)S(1)}, f32[3,4,1024]{2,1,0:T(4,128)}, u32[]{:S(2)}) copy-start(f32[3,4,1024]{2,1,0:T(4,128)} %taps_ref.5) | copy-start | bytes 147460
  0.0 33.8 %copy-start.5 = (f32[3,1024]{1,0:T(4,128)S(1)}, f32[3,1024]{1,0:T(4,128)}, u32[]{:S(2)}) copy-start(f32[3,1024]{1,0:T(4,128)} %ogain_ref.5) | copy-start | bytes 36868
  0.0 33.8 %copy-start.6 = (f32[3,512]{1,0:T(4,128)S(1)}, f32[3,512]{1,0:T(4,128)}, u32[]{:S(2)}) copy-start(f32[3,512]{1,0:T(4,128)} %norm_ref.5) | copy-start | bytes 18436
  0.0 33.8 %copy-start.7 = (f32[3,4,128]{2,1,0:T(4,128)S(1)}, f32[3,4,128]{2,1,0:T(4,128)}, u32[]{:S(2)}) copy-start(f32[3,4,128]{2,1,0:T(4,128)} %ctaps_ref.5) | copy-start | bytes 18436
  0.1 33.8 %copy-start.8 = (f32[3,16]{1,0:T(4,128)S(1)}, f32[3,16]{1,0:T(4,128)}, u32[]{:S(2)}) copy-start(f32[3,16]{1,0:T(4,128)} %bias_ref.5) | copy-start | bytes 580
  0.1 33.8 %copy-start.9 = (f32[3,16]{1,0:T(4,128)S(1)}, f32[3,16]{1,0:T(4,128)}, u32[]{:S(2)}) copy-start(f32[3,16]{1,0:T(4,128)} %rate_ref.5) | copy-start | bytes 580
  0.1 33.8 %copy-start.10 = (f32[3,16]{1,0:T(4,128)S(1)}, f32[3,16]{1,0:T(4,128)}, u32[]{:S(2)}) copy-start(f32[3,16]{1,0:T(4,128)} %skip_ref.5) | copy-start | bytes 580

commit v2 on v1

v2 whole, which is shorter than its diff:
```python
import functools

import jax
import jax.numpy as jnp
from jax import lax
from jax.experimental import pallas as pl
from jax.experimental.pallas import tpu as pltpu
from jax.sharding import PartitionSpec as P

LINES = 8
LENGTH = 64
ROWS = LINES * LENGTH
WIDTH = 512
INNER = 1024
HEADS = 16
STATES = 64
STEPS = 4
CHUNK = INNER // STEPS
LANES = 128
BLOCKS = 1
BLOCK = ROWS // BLOCKS
WHOLE = (True, False, False, False, False, False, True, True, True, True, False)
LOG2E = 1.4426950408889634
F32 = jnp.float32
BF16 = jnp.bfloat16


def iota(shape, dim):
    return lax.broadcasted_iota(jnp.int32, shape, dim)


def dot(a, b):
    return jnp.dot(a, b, preferred_element_type=F32)


def dot_t(a, b):
    return lax.dot_general(a, b, (((1,), (1,)), ((), ())), preferred_element_type=F32)


def split3(value):
    high = value.astype(BF16)
    rest = value - high.astype(F32)
    middle = rest.astype(BF16)
    low = (rest - middle.astype(F32)).astype(BF16)
    return high, middle, low


def swap_matrix():
    r, c = iota((64, 64), 0), iota((64, 64), 1)
    return ((r // 8 == c % 8) & (r % 8 == c // 8)).astype(BF16)


def half_silu(half):
    return half + half * jnp.tanh(half)


def kernel(layer, stride, *refs):
    (x_in, *given) = refs[:12]
    out_ref = refs[12]
    (xf, normed, padded, cpadded, scores, cum, rowside, skipx, gates, gated, sumsq, total_ref) = refs[13:25]
    if layer == 0:
        held, sems = refs[25:37], refs[37]
        sources = [x_in] + [ref if small else ref.at[layer] for ref, small in zip(given, WHOLE)]
        copies = [pltpu.make_async_copy(src, dst, sems.at[n]) for n, (src, dst) in enumerate(zip(sources, held))]
        for n in (0, 1, 3, 4, 6, 7, 8, 9, 5, 10, 2, 11):
            copies[n].start()
        x_ref, *views = held
    else:
        x_ref, views = x_in, [ref if small else ref.at[layer] for ref, small in zip(given, WHOLE)]

    def wait(*which):
        if layer == 0:
            for n in which:
                copies[n].wait()

    norm_ref, w_ref, wcoup_ref, wsteps_ref, taps_ref, ctaps_ref, bias_ref, rate_ref, skip_ref, ogain_ref, wout = views
    pad = 8 if stride == 1 else 24
    span = LENGTH + pad

    row = iota((LENGTH, LANES), 0)
    col = iota((LENGTH, LANES), 1) % LENGTH
    if stride == 1:
        keep = col <= row
    else:
        keep = (col // stride <= row // stride) & (col % stride == row % stride)

    def load_line(s):
        if layer == 0:
            return xf[:, s * 8 : (s + 1) * 8, :].reshape(LENGTH, WIDTH)
        return x_ref[:, s].astype(F32).reshape(LENGTH, WIDTH)

    wait(0, 1)
    if layer == 0:
        swap = swap_matrix()
        for f in range(8):
            xf[f] = dot(swap, x_ref[f].astype(F32).reshape(64, WIDTH).astype(BF16))
    gain = norm_ref[layer : layer + 1, :] * 0.5
    for s in range(LINES):
        x = load_line(s)
        scale = lax.rsqrt(jnp.mean(x * x, axis=-1, keepdims=True) + 1e-05)
        normed[s * LENGTH : (s + 1) * LENGTH, :] = (x * scale * gain).astype(BF16)

    wait(3, 4, 6, 7, 8, 9)
    spread16 = jnp.where(iota((HEADS, LANES), 1) % HEADS == iota((HEADS, LANES), 0), 2.0, 0.0).astype(BF16)
    wsteps = lax.dot_general(
        wsteps_ref[...], spread16, (((0,), (0,)), ((), ())), preferred_element_type=F32
    ).astype(BF16)
    small = dot(normed[...], jnp.concatenate([wcoup_ref[...], wsteps], axis=1))

    for s in range(LINES):
        for t in range(2):
            padded[t, s * span : s * span + pad, :] = jnp.zeros((pad, LANES), F32)
        cpadded[s * span : s * span + pad, :] = jnp.zeros((pad, LANES), F32)
        cpadded[s * span + pad : (s + 1) * span, :] = small[s * LENGTH : (s + 1) * LENGTH, :LANES]
    taps = ctaps_ref[...]
    bias = jnp.concatenate([bias_ref[layer : layer + 1, :]] * 8, axis=1)
    rate = jnp.concatenate([-jnp.exp(rate_ref[layer : layer + 1, :]) * LOG2E] * 8, axis=1)
    tri = keep[:, :LENGTH].astype(BF16)
    tri3 = jnp.concatenate([tri] * 3, axis=1)
    group = iota((LENGTH, LANES), 1) // HEADS
    raw = small[:LENGTH, LANES:]
    for s in range(1, LINES):
        raw = jnp.where(group == s, small[s * LENGTH : (s + 1) * LENGTH, LANES:], raw)
    raw = raw + bias
    e = jnp.exp(-jnp.abs(raw))
    steps = jnp.maximum(raw, 0.0) + jnp.where(e < 1e-3, e - 0.5 * e * e, jnp.log(1.0 + e))
    total = dot(tri3, jnp.concatenate(split3(steps * rate), axis=0))
    high, middle, low = (part.astype(F32) for part in split3(total))
    middle = pltpu.roll(middle, HEADS, 1)
    low = pltpu.roll(low, 2 * HEADS, 1)
    for s in range(LINES):
        parts = jnp.where(
            group == s,
            high,
            jnp.where(group == (s + 1) % 8, middle, jnp.where(group == (s + 2) % 8, low, 0.0)),
        )
        cum[s * LENGTH : (s + 1) * LENGTH, :] = parts.astype(BF16)
    side = total - jnp.log(steps) * LOG2E
    turned = jnp.transpose(jnp.concatenate([side, side], axis=0))
    for s in range(LINES):
        rowside[s] = turned[s * HEADS : (s + 1) * HEADS, :]
    for s in range(LINES):
        base = s * span + pad
        half = sum(
            cpadded[base - (3 - k) * stride : base - (3 - k) * stride + LENGTH, :] * taps[k : k + 1, :]
            for k in range(4)
        )
        maps = half_silu(half)
        inputs = maps[:, :STATES].astype(BF16)
        outputs = maps[:, STATES:].astype(BF16)
        scores[s] = dot_t(outputs, jnp.concatenate([inputs, inputs], axis=0))

    spread = (iota((HEADS, INNER), 1) // STATES == iota((HEADS, INNER), 0)).astype(F32)
    skip = jnp.dot(
        jnp.broadcast_to(skip_ref[layer : layer + 1, :], (8, HEADS)),
        spread,
        precision=lax.Precision.HIGHEST,
        preferred_element_type=F32,
    )
    for c in range(STEPS):
        skipx[c] = skip[:, c * CHUNK : (c + 1) * CHUNK]
    sumsq[...] = jnp.zeros_like(sumsq)
    total_ref[...] = jnp.zeros_like(total_ref)
    gated[1] = jnp.zeros((ROWS, CHUNK), BF16)
    wait(5, 10, 2, 11)

    def project(c, slot, rows):
        first = pl.multiple_of(c * CHUNK, CHUNK)
        return dot(gated[slot, rows, :], wout[pl.ds(first, CHUNK), :])

    def chunk(j, carry):
        start = pl.multiple_of(j * CHUNK, CHUNK)
        lane3 = iota((LANES, CHUNK), 0)
        expand = (lane3 % HEADS == 4 * j + iota((LANES, CHUNK), 1) // STATES).astype(BF16)
        taps = taps_ref[:, pl.ds(start, CHUNK)]
        ogain = ogain_ref[layer : layer + 1, pl.ds(start, CHUNK)]
        wgate = w_ref[:, pl.ds(start, CHUNK)]
        wvalue = w_ref[:, pl.ds(pl.multiple_of(INNER + j * CHUNK, CHUNK), CHUNK)]
        lower = iota((LENGTH, LANES), 1) < STATES
        lower1 = iota((1, LANES), 1) < STATES
        zero = jnp.zeros((LENGTH, LANES), BF16)
        slot = lax.rem(j, 2)
        before = lax.rem(j + 1, 2)
        for b in range(BLOCKS):
            rows = slice(b * BLOCK, (b + 1) * BLOCK)
            value = dot(normed[rows, :], wvalue)
            for q in range(BLOCK // LENGTH):
                s = b * (BLOCK // LENGTH) + q
                for t in range(2):
                    padded[t, s * span + pad : (s + 1) * span, :] = value[
                        q * LENGTH : (q + 1) * LENGTH, t * LANES : (t + 1) * LANES
                    ]
            gates[rows, :] = half_silu(dot(normed[rows, :], wgate))
            time_side = dot(cum[rows, :], expand)
            total_ref[rows, :] += project(jnp.maximum(j - 1, 0), before, rows)
            for q in range(BLOCK // LENGTH):
                s = b * (BLOCK // LENGTH) + q
                here = slice(s * LENGTH, (s + 1) * LENGTH)
                base = s * span + pad
                square = sumsq[here, :]
                for t in range(2):
                    lanes = slice(t * LANES, (t + 1) * LANES)
                    half = sum(
                        padded[t, base - (3 - k) * stride : base - (3 - k) * stride + LENGTH, :] * taps[k : k + 1, lanes]
                        for k in range(4)
                    )
                    silu = half_silu(half)
                    xs = silu.astype(BF16)
                    head = 4 * j + 2 * t
                    side = jnp.where(lower1, rowside[s, pl.ds(head, 1), :], rowside[s, pl.ds(head + 1, 1), :])
                    power = jnp.where(keep, time_side[q * LENGTH : (q + 1) * LENGTH, lanes] - side, -jnp.inf)
                    weights = (scores[s] * jnp.exp2(power)).astype(BF16)
                    pair = jnp.concatenate([jnp.where(lower, xs, zero), jnp.where(lower, zero, xs)], axis=0)
                    mixed = dot(weights, pair) + skipx[j, 0:1, lanes] * silu
                    mixed = mixed * gates[here, lanes]
                    square = square + mixed * mixed
                    gated[slot, here, lanes] = (mixed * ogain[:, lanes]).astype(BF16)
                sumsq[here, :] = square
        return carry

    lax.fori_loop(0, STEPS, chunk, 0)

    for b in range(BLOCKS):
        rows = slice(b * BLOCK, (b + 1) * BLOCK)
        update = total_ref[rows, :] + project(STEPS - 1, (STEPS - 1) % 2, rows)
        scale = lax.rsqrt(jnp.sum(sumsq[rows, :], axis=-1, keepdims=True) * (1.0 / INNER) + 1e-05)
        update = update * scale
        for q in range(BLOCK // LENGTH):
            s = b * (BLOCK // LENGTH) + q
            y = load_line(s) + update[q * LENGTH : (q + 1) * LENGTH, :]
            if layer == 0:
                out_ref[:, s] = y.reshape(8, 8, WIDTH).astype(BF16)
            elif layer == 1:
                xf[:, s * 8 : (s + 1) * 8, :] = y.reshape(8, 8, WIDTH)
            else:
                out_ref[s] = y.reshape(8, 8, WIDTH).astype(BF16)
    if layer == 1:
        swap = swap_matrix()
        for i in range(8):
            turned = dot(swap, xf[i].astype(BF16))
            out_ref[:, i] = turned.reshape(8, 8, WIDTH).astype(BF16)


def mixer(x, layer, params):
    stride = 8 if layer == 0 else 1
    pad = 8 if stride == 1 else 24
    span = LENGTH + pad
    scratch = [
        pltpu.VMEM((8, 64, WIDTH), F32),
        pltpu.VMEM((ROWS, WIDTH), BF16),
        pltpu.VMEM((2, LINES * span, LANES), F32),
        pltpu.VMEM((LINES * span, LANES), F32),
        pltpu.VMEM((LINES, LENGTH, LANES), F32),
        pltpu.VMEM((ROWS, LANES), BF16),
        pltpu.VMEM((LINES, HEADS, LANES), F32),
        pltpu.VMEM((STEPS, 8, CHUNK), F32),
        pltpu.VMEM((ROWS, CHUNK), F32),
        pltpu.VMEM((2, ROWS, CHUNK), BF16),
        pltpu.VMEM((ROWS, LANES), F32),
        pltpu.VMEM((ROWS, WIDTH), F32),
    ]
    space = pltpu.VMEM
    if layer == 0:
        space = pl.ANY
        x, *params = (pltpu.with_memory_space_constraint(p, pltpu.HBM) for p in (x, *params))
        shapes = [p.shape if small else p.shape[1:] for p, small in zip(params, WHOLE)]
        scratch += [pltpu.VMEM(x.shape, BF16)] + [pltpu.VMEM(shape, p.dtype) for shape, p in zip(shapes, params)]
        scratch += [pltpu.SemaphoreType.DMA((12,))]
    return pl.pallas_call(
        functools.partial(kernel, layer, stride),
        in_specs=[pl.BlockSpec(memory_space=space)] * 12,
        out_specs=pl.BlockSpec(memory_space=pltpu.VMEM),
        out_shape=jax.ShapeDtypeStruct((8, 8, 8, WIDTH), BF16),
        scratch_shapes=scratch,
        name=f"mixer{layer}",
        compiler_params=pltpu.CompilerParams(vmem_limit_bytes=24 * 2**20),
        cost_estimate=pl.CostEstimate(flops=2_000_000_000, bytes_accessed=5_000_000, transcendentals=2_000_000),
    )(x, *params)


def shards(tokens, *params):
    params = params[:3] + (jnp.swapaxes(params[3], 1, 2),) + params[4:]
    current = mixer(tokens, 0, params)
    current = lax.all_to_all(current, "ha", split_axis=0, concat_axis=0, tiled=True)
    current = mixer(current, 1, params)
    current = lax.all_to_all(current, "wa", split_axis=0, concat_axis=0, tiled=True)
    current = mixer(current, 2, params)
    current = current.reshape(64, 8, WIDTH)
    current = lax.all_to_all(current, ("ha", "wa"), split_axis=0, concat_axis=0, tiled=True)
    return current.reshape(8, 8, 8, WIDTH)


def solution(mesh):
    spec = P("ba", "ha", "wa", None)
    return jax.shard_map(shards, mesh=mesh, in_specs=(spec,) + (P(),) * 11, out_specs=spec, check_vma=False)
```

time: 83.4 us -> 80.7 us (0.968)
  Pallas kernels: 19.9 us -> 17.1 us
    pallas_call x3, Pallas kernels: 19.9 us -> 17.1 us  [mixer(): pl.pallas_call(functools.partial(kernel, layer, stride), in_specs=[pl.Blo...]
where the time goes in v2:
time: 80.7 us; the launch traced here: 80.6 us
  blocking collectives  62.5 us (77%)
  Pallas kernels  17.1 us (21%)
  local copies, waits for them, and re-layouts  0.84 us (1%)
    all_to_all x1, blocking collectives, shards(): lax.all_to_all(current, 'ha', split_axis=0, concat_axis=0, tiled=True)  26.3 us
    all_to_all x1, blocking collectives, shards(): lax.all_to_all(current, ('ha', 'wa'), split_axis=0, concat_axis=0, tiled=...  23.2 us
    pallas_call x3, Pallas kernels, mixer(): pl.pallas_call(functools.partial(kernel, layer, stride), in_specs=[pl.Blo...  17.1 us
    all_to_all x1, blocking collectives, shards(): lax.all_to_all(current, 'wa', split_axis=0, concat_axis=0, tiled=True)  13 us

profile of v2, /device:TPU:4, one launch (start us, length us, event | category | flops | bytes accessed | tf_op | source)
XLA Modules:
  0.0 80.6 jit_solution(11682563705624642824)
XLA Ops:
  0.0 0.0 copy-start
  0.0 0.0 copy-start.4
  0.0 0.0 copy-start.9
  0.0 0.0 copy-start.8
  0.0 0.0 copy-start.7
  0.0 0.0 copy-start.6
  0.0 0.0 copy-start.3
  0.0 0.0 copy-start.1
  0.1 0.0 slice-start
  0.1 0.0 copy-start.5
  0.1 0.0 copy-start.2
  0.1 0.0 slice-start.1
  0.1 6.6 %mixer0.1 = bf16[8,8,8,512]{3,2,1,0:T(8,128)(2,1)S(1)} custom-call(bf16[8,8,8,512]{3,2,1,0:T(8,128)(2,1)} %refs_0_.1, f32[3,512]{1,0:T(4,128)} %refs_1_.5, bf16[3,512,2048]{2,1,0:T(8,128)(2,1)} %refs_2_.5, bf16[3,512,128]{2,1,0:T(8,128)(2,1)} %refs_3_.5, bf16[3,16,512]{2,1,0:T(8,128)(2,1)} %bitcast.6, f32[3,4,1024]{2,1,0:T(4,128)} %refs_5_.5, ...), custom_call_target="tpu_custom_call" | custom-call | flops 2000000000 | bytes 5000000 | tf_op jit(solution)/shard_map/mixer0/pallas_call | solution.py:269
  6.7 26.3 %all_to_all.15.refs_0_ = bf16[8,8,8,512]{3,2,1,0:T(8,128)(2,1)S(1)} all-to-all(bf16[8,8,8,512]{3,2,1,0:T(8,128)(2,1)S(1)} %mixer0.1), channel_id=1, replica_groups=mesh['ha'=8,'wa'=8,'ba'=4] {'ha'}, dimensions={0} | all-to-all | bytes 1048576 | tf_op jit(solution)/shard_map/all_to_all | solution.py:284
  33.0 0.0 copy-done
  33.0 0.0 copy-done.4
  33.0 0.0 copy-done.9
  33.0 0.0 copy-done.8
  33.0 0.0 copy-done.7
  33.0 0.0 copy-done.6
  33.1 0.0 copy-done.3
  33.1 0.0 copy-done.1
  33.1 0.0 slice-done
  33.1 0.0 copy-done.5
  33.1 0.0 copy-done.2
  33.1 0.0 slice-done.1
  33.1 5.3 %mixer1.1 = bf16[8,8,8,512]{3,2,1,0:T(8,128)(2,1)S(1)} custom-call(bf16[8,8,8,512]{3,2,1,0:T(8,128)(2,1)S(1)} %all_to_all.15.refs_0_, f32[3,512]{1,0:T(4,128)S(1)} %copy-done.5, bf16[3,512,2048]{2,1,0:T(8,128)(2,1)S(1)} %bitcast.4, bf16[3,512,128]{2,1,0:T(8,128)(2,1)S(1)} %copy-done.1, bf16[3,16,512]{2,1,0:T(8,128)(2,1)S(1)} %bitcast.7, ...), custom_call_target="tpu_custom_call" | custom-call | flops 2000000000 | bytes 5000000 | tf_op jit(solution)/shard_map/mixer1/pallas_call | solution.py:269
  38.5 13.0 %all_to_all.16.refs_0_ = bf16[8,8,8,512]{3,2,1,0:T(8,128)(2,1)S(1)} all-to-all(bf16[8,8,8,512]{3,2,1,0:T(8,128)(2,1)S(1)} %mixer1.1), channel_id=1, replica_groups=mesh['ha'=8,'wa'=8,'ba'=4] {'wa'}, dimensions={0} | all-to-all | bytes 1048576 | tf_op jit(solution)/shard_map/all_to_all | solution.py:286
  51.5 5.1 %mixer2.1 = bf16[8,8,8,512]{3,2,1,0:T(8,128)(2,1)S(1)} custom-call(bf16[8,8,8,512]{3,2,1,0:T(8,128)(2,1)S(1)} %all_to_all.16.refs_0_, f32[3,512]{1,0:T(4,128)S(1)} %copy-done.5, bf16[3,512,2048]{2,1,0:T(8,128)(2,1)S(1)} %bitcast.4, bf16[3,512,128]{2,1,0:T(8,128)(2,1)S(1)} %copy-done.1, bf16[3,16,512]{2,1,0:T(8,128)(2,1)S(1)} %bitcast.8, ...), custom_call_target="tpu_custom_call" | custom-call | flops 2000000000 | bytes 5000000 | tf_op jit(solution)/shard_map/mixer2/pallas_call | solution.py:269
  56.6 23.2 %all_to_all.17 = bf16[64,8,512]{2,1,0:T(8,128)(2,1)S(1)} all-to-all(bf16[64,8,512]{2,1,0:T(8,128)(2,1)S(1)} %bitcast.5), channel_id=1, replica_groups=mesh['ha'=8,'wa'=8,'ba'=4] {'ha','wa'}, dimensions={0} | all-to-all | bytes 1048576 | tf_op jit(solution)/shard_map/all_to_all | solution.py:289
  79.8 0.8 copy.14
  (1 shorter events, 0.0 us)
Async XLA Ops:
  0.0 33.0 %copy-start = (bf16[3,1024,512]{2,1,0:T(8,128)(2,1)S(1)}, bf16[3,1024,512]{2,1,0:T(8,128)(2,1)}, u32[]{:S(2)}) copy-start(bf16[3,1024,512]{2,1,0:T(8,128)(2,1)} %refs_11_.5) | copy-start | bytes 9437188
  0.0 33.0 %copy-start.4 = (f32[3,1024]{1,0:T(4,128)S(1)}, f32[3,1024]{1,0:T(4,128)}, u32[]{:S(2)}) copy-start(f32[3,1024]{1,0:T(4,128)} %refs_10_.5) | copy-start | bytes 36868
  0.0 33.0 %copy-start.9 = (f32[3,16]{1,0:T(4,128)S(1)}, f32[3,16]{1,0:T(4,128)}, u32[]{:S(2)}) copy-start(f32[3,16]{1,0:T(4,128)} %refs_9_.5) | copy-start | bytes 580
  0.0 33.0 %copy-start.8 = (f32[3,16]{1,0:T(4,128)S(1)}, f32[3,16]{1,0:T(4,128)}, u32[]{:S(2)}) copy-start(f32[3,16]{1,0:T(4,128)} %refs_8_.5) | copy-start | bytes 580
  0.0 33.0 %copy-start.7 = (f32[3,16]{1,0:T(4,128)S(1)}, f32[3,16]{1,0:T(4,128)}, u32[]{:S(2)}) copy-start(f32[3,16]{1,0:T(4,128)} %refs_7_.5) | copy-start | bytes 580
  0.0 33.0 %copy-start.6 = (f32[3,4,128]{2,1,0:T(4,128)S(1)}, f32[3,4,128]{2,1,0:T(4,128)}, u32[]{:S(2)}) copy-start(f32[3,4,128]{2,1,0:T(4,128)} %refs_6_.5) | copy-start | bytes 18436
  0.0 33.0 %copy-start.3 = (f32[3,4,1024]{2,1,0:T(4,128)S(1)}, f32[3,4,1024]{2,1,0:T(4,128)}, u32[]{:S(2)}) copy-start(f32[3,4,1024]{2,1,0:T(4,128)} %refs_5_.5) | copy-start | bytes 147460
  0.0 33.0 %copy-start.1 = (bf16[3,512,128]{2,1,0:T(8,128)(2,1)S(1)}, bf16[3,512,128]{2,1,0:T(8,128)(2,1)}, u32[]{:S(2)}) copy-start(bf16[3,512,128]{2,1,0:T(8,128)(2,1)} %refs_3_.5) | copy-start | bytes 1179652
  0.1 33.0 %slice-start = ((s8[6291456]{0:T(1024)(128)(4,1)}), s8[4194304]{0:T(1024)(128)(4,1)S(1)}, s32[]{:S(2)}) async-start(s8[6291456]{0:T(1024)(128)(4,1)} %bitcast.3), calls=%async_computation.3 | async-start | bytes 8388608
  0.1 33.0 %copy-start.5 = (f32[3,512]{1,0:T(4,128)S(1)}, f32[3,512]{1,0:T(4,128)}, u32[]{:S(2)}) copy-start(f32[3,512]{1,0:T(4,128)} %refs_1_.5) | copy-start | bytes 18436
  0.1 33.0 %copy-start.2 = (bf16[3,512,16]{1,2,0:T(8,128)(2,1)S(1)}, bf16[3,512,16]{1,2,0:T(8,128)(2,1)}, u32[]{:S(2)}) copy-start(bf16[3,512,16]{1,2,0:T(8,128)(2,1)} %param.16) | copy-start | bytes 147460
  0.1 33.0 %slice-start.1 = ((s8[6291456]{0:T(1024)(128)(4,1)}), s8[2097152]{0:T(1024)(128)(4,1)S(1)}, s32[]{:S(2)}) async-start(s8[6291456]{0:T(1024)(128)(4,1)} %bitcast.3), calls=%async_computation.4 | async-start | bytes 4194304

commit v3 on v2

--- a/solution.py
+++ b/solution.py
@@ -5,6 +5,7 @@
 from jax import lax
 from jax.experimental import pallas as pl
 from jax.experimental.pallas import tpu as pltpu
+from jax.sharding import Mesh
 from jax.sharding import PartitionSpec as P
 
 LINES = 8
@@ -19,6 +20,7 @@
 LANES = 128
 BLOCKS = 1
 BLOCK = ROWS // BLOCKS
+GIVEN = ((4, 2, 2, 4), (2, 4, 4, 2), (4, 2, 4, 2))
 WHOLE = (True, False, False, False, False, False, True, True, True, True, False)
 LOG2E = 1.4426950408889634
 F32 = jnp.float32
@@ -48,6 +50,11 @@
 def swap_matrix():
     r, c = iota((64, 64), 0), iota((64, 64), 1)
     return ((r // 8 == c % 8) & (r % 8 == c // 8)).astype(BF16)
+
+
+def order_matrix():
+    r, c = iota((64, 64), 0), iota((64, 64), 1)
+    return (c == (r // 4 % 2) * 32 + (r // 8 % 4) * 8 + (r // 32) * 4 + r % 4).astype(BF16)
 
 
 def half_silu(half):
@@ -87,9 +94,24 @@
     def load_line(s):
         if layer == 0:
             return xf[:, s * 8 : (s + 1) * 8, :].reshape(LENGTH, WIDTH)
-        return x_ref[:, s].astype(F32).reshape(LENGTH, WIDTH)
+        if layer == 1:
+            return x_ref[:, :, s // 4, s % 4].astype(F32).reshape(LENGTH, WIDTH)
+        return xf[s]
+
+    for s in range(LINES):
+        for t in range(2):
+            padded[t, s * span : s * span + pad, :] = jnp.zeros((pad, LANES), F32)
+        cpadded[s * span : s * span + pad, :] = jnp.zeros((pad, LANES), F32)
+    sumsq[...] = jnp.zeros_like(sumsq)
+    total_ref[...] = jnp.zeros_like(total_ref)
+    gated[1] = jnp.zeros((ROWS, CHUNK), BF16)
 
     wait(0, 1)
+    if layer == 2:
+        order = order_matrix()
+        for s in range(LINES):
+            line = x_ref[:, :, s // 2, s % 2].astype(F32).reshape(LENGTH, WIDTH)
+            xf[s] = dot(order, line.astype(BF16))
     if layer == 0:
         swap = swap_matrix()
         for f in range(8):
@@ -108,9 +130,6 @@
     small = dot(normed[...], jnp.concatenate([wcoup_ref[...], wsteps], axis=1))
 
     for s in range(LINES):
-        for t in range(2):
-            padded[t, s * span : s * span + pad, :] = jnp.zeros((pad, LANES), F32)
-        cpadded[s * span : s * span + pad, :] = jnp.zeros((pad, LANES), F32)
         cpadded[s * span + pad : (s + 1) * span, :] = small[s * LENGTH : (s + 1) * LENGTH, :LANES]
     taps = ctaps_ref[...]
     bias = jnp.concatenate([bias_ref[layer : layer + 1, :]] * 8, axis=1)
@@ -159,9 +178,6 @@
     )
     for c in range(STEPS):
         skipx[c] = skip[:, c * CHUNK : (c + 1) * CHUNK]
-    sumsq[...] = jnp.zeros_like(sumsq)
-    total_ref[...] = jnp.zeros_like(total_ref)
-    gated[1] = jnp.zeros((ROWS, CHUNK), BF16)
     wait(5, 10, 2, 11)
 
     def project(c, slot, rows):
@@ -229,16 +245,16 @@
             s = b * (BLOCK // LENGTH) + q
             y = load_line(s) + update[q * LENGTH : (q + 1) * LENGTH, :]
             if layer == 0:
-                out_ref[:, s] = y.reshape(8, 8, WIDTH).astype(BF16)
+                out_ref[:, s // 4, :, s % 4] = y.reshape(4, 2, 8, WIDTH).astype(BF16)
             elif layer == 1:
                 xf[:, s * 8 : (s + 1) * 8, :] = y.reshape(8, 8, WIDTH)
             else:
-                out_ref[s] = y.reshape(8, 8, WIDTH).astype(BF16)
+                out_ref[s // 2, :, :, s % 2] = y.reshape(2, 4, 8, WIDTH).astype(BF16)
     if layer == 1:
         swap = swap_matrix()
         for i in range(8):
             turned = dot(swap, xf[i].astype(BF16))
-            out_ref[:, i] = turned.reshape(8, 8, WIDTH).astype(BF16)
+            out_ref[i % 2, :, i // 2] = turned.reshape(4, 2, 8, WIDTH).astype(BF16)
 
 
 def mixer(x, layer, params):
@@ -270,7 +286,7 @@
         functools.partial(kernel, layer, stride),
         in_specs=[pl.BlockSpec(memory_space=space)] * 12,
         out_specs=pl.BlockSpec(memory_space=pltpu.VMEM),
-        out_shape=jax.ShapeDtypeStruct((8, 8, 8, WIDTH), BF16),
+        out_shape=jax.ShapeDtypeStruct(GIVEN[layer] + (8, WIDTH), BF16),
         scratch_shapes=scratch,
         name=f"mixer{layer}",
         compiler_params=pltpu.CompilerParams(vmem_limit_bytes=24 * 2**20),
@@ -280,16 +296,16 @@
 
 def shards(tokens, *params):
     params = params[:3] + (jnp.swapaxes(params[3], 1, 2),) + params[4:]
-    current = mixer(tokens, 0, params)
-    current = lax.all_to_all(current, "ha", split_axis=0, concat_axis=0, tiled=True)
-    current = mixer(current, 1, params)
-    current = lax.all_to_all(current, "wa", split_axis=0, concat_axis=0, tiled=True)
-    current = mixer(current, 2, params)
-    current = current.reshape(64, 8, WIDTH)
-    current = lax.all_to_all(current, ("ha", "wa"), split_axis=0, concat_axis=0, tiled=True)
+    current = tokens
+    for layer, axes in enumerate((("zh", "core", "zl"), ("core", "y"), ("zh", "zl", "y"))):
+        current = mixer(current, layer, params)
+        shape = current.shape
+        current = current.reshape(lax.axis_size(axes), -1, WIDTH)
+        current = lax.all_to_all(current, axes, split_axis=0, concat_axis=0, tiled=True).reshape(shape)
     return current.reshape(8, 8, 8, WIDTH)
 
 
 def solution(mesh):
-    spec = P("ba", "ha", "wa", None)
+    mesh = Mesh(mesh.devices.reshape(4, 2, 2, 4, 4), ("zh", "core", "zl", "y", "x"))
+    spec = P("x", ("zh", "core"), ("zl", "y"), None)
     return jax.shard_map(shards, mesh=mesh, in_specs=(spec,) + (P(),) * 11, out_specs=spec, check_vma=False)

time: 80.7 us -> 79.6 us (0.986)
  blocking collectives: 62.5 us -> 61.2 us
    all_to_all x3, blocking collectives: 62.5 us -> 61.2 us  [shards(): lax.all_to_all(current, axes, split_axis=0, concat_axis=0, tiled=True)]
where the time goes in v3:
time: 79.6 us; the launch traced here: 79.4 us
  blocking collectives  61.2 us (77%)
  Pallas kernels  17.1 us (21%)
  local copies, waits for them, and re-layouts  0.84 us (1%)
    all_to_all x3, blocking collectives, shards(): lax.all_to_all(current, axes, split_axis=0, concat_axis=0, tiled=True)  61.2 us
    pallas_call x3, Pallas kernels, mixer(): pl.pallas_call(functools.partial(kernel, layer, stride), in_specs=[pl.Blo...  17.1 us

profile of v3, /device:TPU:4, one launch (start us, length us, event | category | flops | bytes accessed | tf_op | source)
XLA Modules:
  0.0 79.4 jit_solution(3778203075368235478)
XLA Ops:
  0.0 0.0 copy-start
  0.0 0.0 copy-start.4
  0.0 0.0 copy-start.9
  0.0 0.0 copy-start.8
  0.0 0.0 copy-start.7
  0.0 0.0 copy-start.6
  0.0 0.0 copy-start.3
  0.0 0.0 copy-start.1
  0.1 0.0 slice-start
  0.1 0.0 copy-start.5
  0.1 0.0 copy-start.2
  0.1 0.0 slice-start.1
  0.1 6.6 %mixer0.1 = bf16[4,2,2,4,8,512]{5,4,3,2,1,0:T(8,128)(2,1)S(1)} custom-call(bf16[8,8,8,512]{3,2,1,0:T(8,128)(2,1)} %refs_0_.1, f32[3,512]{1,0:T(4,128)} %refs_1_.5, bf16[3,512,2048]{2,1,0:T(8,128)(2,1)} %refs_2_.5, bf16[3,512,128]{2,1,0:T(8,128)(2,1)} %refs_3_.5, bf16[3,16,512]{2,1,0:T(8,128)(2,1)} %bitcast.14, f32[3,4,1024]{2,1,0:T(4,128)} %refs_5_.5, ...), custom_call_target="tpu_custom_call" | custom-call | flops 2000000000 | bytes 5000000 | tf_op jit(solution)/shard_map/mixer0/pallas_call | solution.py:285
  6.7 23.8 %all_to_all.15 = bf16[16,32,512]{2,1,0:T(8,128)(2,1)S(1)} all-to-all(bf16[16,32,512]{2,1,0:T(8,128)(2,1)S(1)} %bitcast.13), channel_id=1, replica_groups=mesh['zh'=4,'core'=2,'zl'=2,'y'=4,'x'=4] {'zh','core','zl'}, dimensions={0} | all-to-all | bytes 1048576 | tf_op jit(solution)/shard_map/all_to_all | solution.py:304
  30.5 0.0 copy-done
  30.5 0.0 copy-done.4
  30.5 0.0 copy-done.9
  30.5 0.0 copy-done.8
  30.6 0.0 copy-done.7
  30.6 0.0 copy-done.6
  30.6 0.0 copy-done.3
  30.6 0.0 copy-done.1
  30.6 0.0 slice-done
  30.6 0.0 copy-done.5
  30.6 0.0 copy-done.2
  30.6 0.0 slice-done.1
  30.6 5.3 %mixer1.1 = bf16[2,4,4,2,8,512]{5,4,3,2,1,0:T(8,128)(2,1)S(1)} custom-call(bf16[4,2,2,4,8,512]{5,4,3,2,1,0:T(8,128)(2,1)S(1)} %bitcast.9, f32[3,512]{1,0:T(4,128)S(1)} %copy-done.5, bf16[3,512,2048]{2,1,0:T(8,128)(2,1)S(1)} %bitcast.8, bf16[3,512,128]{2,1,0:T(8,128)(2,1)S(1)} %copy-done.1, bf16[3,16,512]{2,1,0:T(8,128)(2,1)S(1)} %bitcast.15, ...), custom_call_target="tpu_custom_call" | custom-call | flops 2000000000 | bytes 5000000 | tf_op jit(solution)/shard_map/mixer1/pallas_call | solution.py:285
  36.0 14.0 %all_to_all.16 = bf16[8,64,512]{2,1,0:T(8,128)(2,1)S(1)} all-to-all(bf16[8,64,512]{2,1,0:T(8,128)(2,1)S(1)} %bitcast.10), channel_id=1, replica_groups=mesh['zh'=4,'core'=2,'zl'=2,'y'=4,'x'=4] {'core','y'}, dimensions={0} | all-to-all | bytes 1048576 | tf_op jit(solution)/shard_map/all_to_all | solution.py:304
  50.0 5.2 %mixer2.1 = bf16[4,2,4,2,8,512]{5,4,3,2,1,0:T(8,128)(2,1)S(1)} custom-call(bf16[2,4,4,2,8,512]{5,4,3,2,1,0:T(8,128)(2,1)S(1)} %bitcast.11, f32[3,512]{1,0:T(4,128)S(1)} %copy-done.5, bf16[3,512,2048]{2,1,0:T(8,128)(2,1)S(1)} %bitcast.8, bf16[3,512,128]{2,1,0:T(8,128)(2,1)S(1)} %copy-done.1, bf16[3,16,512]{2,1,0:T(8,128)(2,1)S(1)} %bitcast.16, ...), custom_call_target="tpu_custom_call" | custom-call | flops 2000000000 | bytes 5000000 | tf_op jit(solution)/shard_map/mixer2/pallas_call | solution.py:285
  55.2 23.3 %all_to_all.17 = bf16[32,16,512]{2,1,0:T(8,128)(2,1)S(1)} all-to-all(bf16[32,16,512]{2,1,0:T(8,128)(2,1)S(1)} %bitcast.12), channel_id=1, replica_groups=mesh['zh'=4,'core'=2,'zl'=2,'y'=4,'x'=4] {'zh','zl','y'}, dimensions={0} | all-to-all | bytes 1048576 | tf_op jit(solution)/shard_map/all_to_all | solution.py:304
  78.6 0.8 copy.14
  (1 shorter events, 0.0 us)
Async XLA Ops:
  0.0 30.5 %copy-start = (bf16[3,1024,512]{2,1,0:T(8,128)(2,1)S(1)}, bf16[3,1024,512]{2,1,0:T(8,128)(2,1)}, u32[]{:S(2)}) copy-start(bf16[3,1024,512]{2,1,0:T(8,128)(2,1)} %refs_11_.5) | copy-start | bytes 9437188
  0.0 30.5 %copy-start.4 = (f32[3,1024]{1,0:T(4,128)S(1)}, f32[3,1024]{1,0:T(4,128)}, u32[]{:S(2)}) copy-start(f32[3,1024]{1,0:T(4,128)} %refs_10_.5) | copy-start | bytes 36868
  0.0 30.5 %copy-start.9 = (f32[3,16]{1,0:T(4,128)S(1)}, f32[3,16]{1,0:T(4,128)}, u32[]{:S(2)}) copy-start(f32[3,16]{1,0:T(4,128)} %refs_9_.5) | copy-start | bytes 580
  0.0 30.5 %copy-start.8 = (f32[3,16]{1,0:T(4,128)S(1)}, f32[3,16]{1,0:T(4,128)}, u32[]{:S(2)}) copy-start(f32[3,16]{1,0:T(4,128)} %refs_8_.5) | copy-start | bytes 580
  0.0 30.5 %copy-start.7 = (f32[3,16]{1,0:T(4,128)S(1)}, f32[3,16]{1,0:T(4,128)}, u32[]{:S(2)}) copy-start(f32[3,16]{1,0:T(4,128)} %refs_7_.5) | copy-start | bytes 580
  0.0 30.5 %copy-start.6 = (f32[3,4,128]{2,1,0:T(4,128)S(1)}, f32[3,4,128]{2,1,0:T(4,128)}, u32[]{:S(2)}) copy-start(f32[3,4,128]{2,1,0:T(4,128)} %refs_6_.5) | copy-start | bytes 18436
  0.0 30.5 %copy-start.3 = (f32[3,4,1024]{2,1,0:T(4,128)S(1)}, f32[3,4,1024]{2,1,0:T(4,128)}, u32[]{:S(2)}) copy-start(f32[3,4,1024]{2,1,0:T(4,128)} %refs_5_.5) | copy-start | bytes 147460
  0.0 30.5 %copy-start.1 = (bf16[3,512,128]{2,1,0:T(8,128)(2,1)S(1)}, bf16[3,512,128]{2,1,0:T(8,128)(2,1)}, u32[]{:S(2)}) copy-start(bf16[3,512,128]{2,1,0:T(8,128)(2,1)} %refs_3_.5) | copy-start | bytes 1179652
  0.1 30.5 %slice-start = ((s8[6291456]{0:T(1024)(128)(4,1)}), s8[4194304]{0:T(1024)(128)(4,1)S(1)}, s32[]{:S(2)}) async-start(s8[6291456]{0:T(1024)(128)(4,1)} %bitcast.7), calls=%async_computation.3 | async-start | bytes 8388608
  0.1 30.5 %copy-start.5 = (f32[3,512]{1,0:T(4,128)S(1)}, f32[3,512]{1,0:T(4,128)}, u32[]{:S(2)}) copy-start(f32[3,512]{1,0:T(4,128)} %refs_1_.5) | copy-start | bytes 18436
  0.1 30.5 %copy-start.2 = (bf16[3,512,16]{1,2,0:T(8,128)(2,1)S(1)}, bf16[3,512,16]{1,2,0:T(8,128)(2,1)}, u32[]{:S(2)}) copy-start(bf16[3,512,16]{1,2,0:T(8,128)(2,1)} %param.16) | copy-start | bytes 147460
  0.1 30.5 %slice-start.1 = ((s8[6291456]{0:T(1024)(128)(4,1)}), s8[2097152]{0:T(1024)(128)(4,1)S(1)}, s32[]{:S(2)}) async-start(s8[6291456]{0:T(1024)(128)(4,1)} %bitcast.7), calls=%async_computation.4 | async-start | bytes 4194304

commit v4 on v3

--- a/solution.py
+++ b/solution.py
@@ -100,7 +100,8 @@
 
     for s in range(LINES):
         for t in range(2):
-            padded[t, s * span : s * span + pad, :] = jnp.zeros((pad, LANES), F32)
+            for slot in range(2):
+                padded[slot, t, s * span : s * span + pad, :] = jnp.zeros((pad, LANES), F32)
         cpadded[s * span : s * span + pad, :] = jnp.zeros((pad, LANES), F32)
     sumsq[...] = jnp.zeros_like(sumsq)
     total_ref[...] = jnp.zeros_like(total_ref)
@@ -129,6 +130,19 @@
     ).astype(BF16)
     small = dot(normed[...], jnp.concatenate([wcoup_ref[...], wsteps], axis=1))
 
+    def produce(c, slot):
+        wgate = w_ref[:, pl.ds(c * CHUNK, CHUNK)]
+        wvalue = w_ref[:, pl.ds(INNER + c * CHUNK, CHUNK)]
+        value = dot(normed[...], wvalue)
+        for s in range(LINES):
+            for t in range(2):
+                padded[slot, t, s * span + pad : (s + 1) * span, :] = value[
+                    s * LENGTH : (s + 1) * LENGTH, t * LANES : (t + 1) * LANES
+                ]
+        gates[slot] = half_silu(dot(normed[...], wgate))
+
+    wait(5, 10, 2, 11)
+    produce(0, 0)
     for s in range(LINES):
         cpadded[s * span + pad : (s + 1) * span, :] = small[s * LENGTH : (s + 1) * LENGTH, :LANES]
     taps = ctaps_ref[...]
@@ -178,37 +192,27 @@
     )
     for c in range(STEPS):
         skipx[c] = skip[:, c * CHUNK : (c + 1) * CHUNK]
-    wait(5, 10, 2, 11)
-
     def project(c, slot, rows):
-        first = pl.multiple_of(c * CHUNK, CHUNK)
+        first = c * CHUNK
         return dot(gated[slot, rows, :], wout[pl.ds(first, CHUNK), :])
 
-    def chunk(j, carry):
-        start = pl.multiple_of(j * CHUNK, CHUNK)
+    def chunk(j, slot):
+        start = j * CHUNK
         lane3 = iota((LANES, CHUNK), 0)
         expand = (lane3 % HEADS == 4 * j + iota((LANES, CHUNK), 1) // STATES).astype(BF16)
         taps = taps_ref[:, pl.ds(start, CHUNK)]
         ogain = ogain_ref[layer : layer + 1, pl.ds(start, CHUNK)]
-        wgate = w_ref[:, pl.ds(start, CHUNK)]
-        wvalue = w_ref[:, pl.ds(pl.multiple_of(INNER + j * CHUNK, CHUNK), CHUNK)]
         lower = iota((LENGTH, LANES), 1) < STATES
         lower1 = iota((1, LANES), 1) < STATES
         zero = jnp.zeros((LENGTH, LANES), BF16)
-        slot = lax.rem(j, 2)
-        before = lax.rem(j + 1, 2)
+        before = 1 - slot
+        if j + 1 < STEPS:
+            produce(j + 1, before)
         for b in range(BLOCKS):
             rows = slice(b * BLOCK, (b + 1) * BLOCK)
-            value = dot(normed[rows, :], wvalue)
-            for q in range(BLOCK // LENGTH):
-                s = b * (BLOCK // LENGTH) + q
-                for t in range(2):
-                    padded[t, s * span + pad : (s + 1) * span, :] = value[
-                        q * LENGTH : (q + 1) * LENGTH, t * LANES : (t + 1) * LANES
-                    ]
-            gates[rows, :] = half_silu(dot(normed[rows, :], wgate))
             time_side = dot(cum[rows, :], expand)
-            total_ref[rows, :] += project(jnp.maximum(j - 1, 0), before, rows)
+            if j > 0:
+                total_ref[rows, :] += project(j - 1, before, rows)
             for q in range(BLOCK // LENGTH):
                 s = b * (BLOCK // LENGTH) + q
                 here = slice(s * LENGTH, (s + 1) * LENGTH)
@@ -217,7 +221,7 @@
                 for t in range(2):
                     lanes = slice(t * LANES, (t + 1) * LANES)
                     half = sum(
-                        padded[t, base - (3 - k) * stride : base - (3 - k) * stride + LENGTH, :] * taps[k : k + 1, lanes]
+                        padded[slot, t, base - (3 - k) * stride : base - (3 - k) * stride + LENGTH, :] * taps[k : k + 1, lanes]
                         for k in range(4)
                     )
                     silu = half_silu(half)
@@ -228,13 +232,13 @@
                     weights = (scores[s] * jnp.exp2(power)).astype(BF16)
                     pair = jnp.concatenate([jnp.where(lower, xs, zero), jnp.where(lower, zero, xs)], axis=0)
                     mixed = dot(weights, pair) + skipx[j, 0:1, lanes] * silu
-                    mixed = mixed * gates[here, lanes]
+                    mixed = mixed * gates[slot, here, lanes]
                     square = square + mixed * mixed
                     gated[slot, here, lanes] = (mixed * ogain[:, lanes]).astype(BF16)
                 sumsq[here, :] = square
-        return carry
-
-    lax.fori_loop(0, STEPS, chunk, 0)
+
+    for j in range(STEPS):
+        chunk(j, j % 2)
 
     for b in range(BLOCKS):
         rows = slice(b * BLOCK, (b + 1) * BLOCK)
@@ -264,13 +268,13 @@
     scratch = [
         pltpu.VMEM((8, 64, WIDTH), F32),
         pltpu.VMEM((ROWS, WIDTH), BF16),
-        pltpu.VMEM((2, LINES * span, LANES), F32),
+        pltpu.VMEM((2, 2, LINES * span, LANES), F32),
         pltpu.VMEM((LINES * span, LANES), F32),
         pltpu.VMEM((LINES, LENGTH, LANES), F32),
         pltpu.VMEM((ROWS, LANES), BF16),
         pltpu.VMEM((LINES, HEADS, LANES), F32),
         pltpu.VMEM((STEPS, 8, CHUNK), F32),
-        pltpu.VMEM((ROWS, CHUNK), F32),
+        pltpu.VMEM((2, ROWS, CHUNK), F32),
         pltpu.VMEM((2, ROWS, CHUNK), BF16),
         pltpu.VMEM((ROWS, LANES), F32),
         pltpu.VMEM((ROWS, WIDTH), F32),

time: 79.6 us -> 76.4 us (0.960)
  Pallas kernels: 17.1 us -> 14 us
    pallas_call x3, Pallas kernels: 17.1 us -> 14 us  [mixer(): pl.pallas_call(functools.partial(kernel, layer, stride), in_specs=[pl.Blo...]
where the time goes in v4:
time: 76.4 us; the launch traced here: 76.2 us
  blocking collectives  61.2 us (80%)
  Pallas kernels  14 us (18%)
  local copies, waits for them, and re-layouts  0.84 us (1%)
    all_to_all x3, blocking collectives, shards(): lax.all_to_all(current, axes, split_axis=0, concat_axis=0, tiled=True)  61.2 us
    pallas_call x3, Pallas kernels, mixer(): pl.pallas_call(functools.partial(kernel, layer, stride), in_specs=[pl.Blo...  14 us

profile of v4, /device:TPU:4, one launch (start us, length us, event | category | flops | bytes accessed | tf_op | source)
XLA Modules:
  0.0 76.2 jit_solution(13388244286963562538)
XLA Ops:
  0.0 0.0 copy-start
  0.0 0.0 copy-start.4
  0.0 0.0 copy-start.9
  0.0 0.0 copy-start.8
  0.0 0.0 copy-start.7
  0.0 0.0 copy-start.6
  0.0 0.0 copy-start.3
  0.0 0.0 copy-start.1
  0.1 0.0 slice-start
  0.1 0.0 copy-start.5
  0.1 0.0 copy-start.2
  0.1 0.0 slice-start.1
  0.1 5.9 %mixer0.1 = bf16[4,2,2,4,8,512]{5,4,3,2,1,0:T(8,128)(2,1)S(1)} custom-call(bf16[8,8,8,512]{3,2,1,0:T(8,128)(2,1)} %refs_0_.1, f32[3,512]{1,0:T(4,128)} %refs_1_.5, bf16[3,512,2048]{2,1,0:T(8,128)(2,1)} %refs_2_.5, bf16[3,512,128]{2,1,0:T(8,128)(2,1)} %refs_3_.5, bf16[3,16,512]{2,1,0:T(8,128)(2,1)} %bitcast.14, f32[3,4,1024]{2,1,0:T(4,128)} %refs_5_.5, ...), custom_call_target="tpu_custom_call" | custom-call | flops 2000000000 | bytes 5000000 | tf_op jit(solution)/shard_map/mixer0/pallas_call | solution.py:289
  6.0 23.8 %all_to_all.15 = bf16[16,32,512]{2,1,0:T(8,128)(2,1)S(1)} all-to-all(bf16[16,32,512]{2,1,0:T(8,128)(2,1)S(1)} %bitcast.13), channel_id=1, replica_groups=mesh['zh'=4,'core'=2,'zl'=2,'y'=4,'x'=4] {'zh','core','zl'}, dimensions={0} | all-to-all | bytes 1048576 | tf_op jit(solution)/shard_map/all_to_all | solution.py:308
  29.8 0.0 copy-done
  29.8 0.0 copy-done.4
  29.8 0.0 copy-done.9
  29.8 0.0 copy-done.8
  29.8 0.0 copy-done.7
  29.8 0.0 copy-done.6
  29.9 0.0 copy-done.3
  29.9 0.0 copy-done.1
  29.9 0.0 slice-done
  29.9 0.0 copy-done.5
  29.9 0.0 copy-done.2
  29.9 0.0 slice-done.1
  29.9 4.1 %mixer1.1 = bf16[2,4,4,2,8,512]{5,4,3,2,1,0:T(8,128)(2,1)S(1)} custom-call(bf16[4,2,2,4,8,512]{5,4,3,2,1,0:T(8,128)(2,1)S(1)} %bitcast.9, f32[3,512]{1,0:T(4,128)S(1)} %copy-done.5, bf16[3,512,2048]{2,1,0:T(8,128)(2,1)S(1)} %bitcast.8, bf16[3,512,128]{2,1,0:T(8,128)(2,1)S(1)} %copy-done.1, bf16[3,16,512]{2,1,0:T(8,128)(2,1)S(1)} %bitcast.15, ...), custom_call_target="tpu_custom_call" | custom-call | flops 2000000000 | bytes 5000000 | tf_op jit(solution)/shard_map/mixer1/pallas_call | solution.py:289
  34.0 14.0 %all_to_all.16 = bf16[8,64,512]{2,1,0:T(8,128)(2,1)S(1)} all-to-all(bf16[8,64,512]{2,1,0:T(8,128)(2,1)S(1)} %bitcast.10), channel_id=1, replica_groups=mesh['zh'=4,'core'=2,'zl'=2,'y'=4,'x'=4] {'core','y'}, dimensions={0} | all-to-all | bytes 1048576 | tf_op jit(solution)/shard_map/all_to_all | solution.py:308
  48.0 4.1 %mixer2.1 = bf16[4,2,4,2,8,512]{5,4,3,2,1,0:T(8,128)(2,1)S(1)} custom-call(bf16[2,4,4,2,8,512]{5,4,3,2,1,0:T(8,128)(2,1)S(1)} %bitcast.11, f32[3,512]{1,0:T(4,128)S(1)} %copy-done.5, bf16[3,512,2048]{2,1,0:T(8,128)(2,1)S(1)} %bitcast.8, bf16[3,512,128]{2,1,0:T(8,128)(2,1)S(1)} %copy-done.1, bf16[3,16,512]{2,1,0:T(8,128)(2,1)S(1)} %bitcast.16, ...), custom_call_target="tpu_custom_call" | custom-call | flops 2000000000 | bytes 5000000 | tf_op jit(solution)/shard_map/mixer2/pallas_call | solution.py:289
  52.1 23.3 %all_to_all.17 = bf16[32,16,512]{2,1,0:T(8,128)(2,1)S(1)} all-to-all(bf16[32,16,512]{2,1,0:T(8,128)(2,1)S(1)} %bitcast.12), channel_id=1, replica_groups=mesh['zh'=4,'core'=2,'zl'=2,'y'=4,'x'=4] {'zh','zl','y'}, dimensions={0} | all-to-all | bytes 1048576 | tf_op jit(solution)/shard_map/all_to_all | solution.py:308
  75.5 0.8 %copy.14 = bf16[8,8,8,512]{3,2,1,0:T(8,128)(2,1)} copy(bf16[8,8,8,512]{3,2,1,0:T(8,128)(2,1)S(1)} %bitcast.17) | data formatting | bytes 1048576
  (1 shorter events, 0.0 us)
Async XLA Ops:
  0.0 29.8 %copy-start = (bf16[3,1024,512]{2,1,0:T(8,128)(2,1)S(1)}, bf16[3,1024,512]{2,1,0:T(8,128)(2,1)}, u32[]{:S(2)}) copy-start(bf16[3,1024,512]{2,1,0:T(8,128)(2,1)} %refs_11_.5) | copy-start | bytes 9437188
  0.0 29.8 %copy-start.4 = (f32[3,1024]{1,0:T(4,128)S(1)}, f32[3,1024]{1,0:T(4,128)}, u32[]{:S(2)}) copy-start(f32[3,1024]{1,0:T(4,128)} %refs_10_.5) | copy-start | bytes 36868
  0.0 29.8 %copy-start.9 = (f32[3,16]{1,0:T(4,128)S(1)}, f32[3,16]{1,0:T(4,128)}, u32[]{:S(2)}) copy-start(f32[3,16]{1,0:T(4,128)} %refs_9_.5) | copy-start | bytes 580
  0.0 29.8 %copy-start.8 = (f32[3,16]{1,0:T(4,128)S(1)}, f32[3,16]{1,0:T(4,128)}, u32[]{:S(2)}) copy-start(f32[3,16]{1,0:T(4,128)} %refs_8_.5) | copy-start | bytes 580
  0.0 29.8 %copy-start.7 = (f32[3,16]{1,0:T(4,128)S(1)}, f32[3,16]{1,0:T(4,128)}, u32[]{:S(2)}) copy-start(f32[3,16]{1,0:T(4,128)} %refs_7_.5) | copy-start | bytes 580
  0.0 29.8 %copy-start.6 = (f32[3,4,128]{2,1,0:T(4,128)S(1)}, f32[3,4,128]{2,1,0:T(4,128)}, u32[]{:S(2)}) copy-start(f32[3,4,128]{2,1,0:T(4,128)} %refs_6_.5) | copy-start | bytes 18436
  0.0 29.8 %copy-start.3 = (f32[3,4,1024]{2,1,0:T(4,128)S(1)}, f32[3,4,1024]{2,1,0:T(4,128)}, u32[]{:S(2)}) copy-start(f32[3,4,1024]{2,1,0:T(4,128)} %refs_5_.5) | copy-start | bytes 147460
  0.0 29.8 %copy-start.1 = (bf16[3,512,128]{2,1,0:T(8,128)(2,1)S(1)}, bf16[3,512,128]{2,1,0:T(8,128)(2,1)}, u32[]{:S(2)}) copy-start(bf16[3,512,128]{2,1,0:T(8,128)(2,1)} %refs_3_.5) | copy-start | bytes 1179652
  0.1 29.8 %slice-start = ((s8[6291456]{0:T(1024)(128)(4,1)}), s8[4194304]{0:T(1024)(128)(4,1)S(1)}, s32[]{:S(2)}) async-start(s8[6291456]{0:T(1024)(128)(4,1)} %bitcast.7), calls=%async_computation.3 | async-start | bytes 8388608
  0.1 29.8 %copy-start.5 = (f32[3,512]{1,0:T(4,128)S(1)}, f32[3,512]{1,0:T(4,128)}, u32[]{:S(2)}) copy-start(f32[3,512]{1,0:T(4,128)} %refs_1_.5) | copy-start | bytes 18436
  0.1 29.8 %copy-start.2 = (bf16[3,512,16]{1,2,0:T(8,128)(2,1)S(1)}, bf16[3,512,16]{1,2,0:T(8,128)(2,1)}, u32[]{:S(2)}) copy-start(bf16[3,512,16]{1,2,0:T(8,128)(2,1)} %param.16) | copy-start | bytes 147460
  0.1 29.8 %slice-start.1 = ((s8[6291456]{0:T(1024)(128)(4,1)}), s8[2097152]{0:T(1024)(128)(4,1)S(1)}, s32[]{:S(2)}) async-start(s8[6291456]{0:T(1024)(128)(4,1)} %bitcast.7), calls=%async_computation.4 | async-start | bytes 4194304
